TPU v7x, 16 devices: a 4x2x1 block of a 4x4x8 slice. The times are simulated.
16 devices in a mesh: dp: 2 (over y, z), pp: 8 (over x, core).
Axes of the slice: x: 4, y: 2, z: 1, core: 2. Of those that a mesh axis runs over, the one named last changes fastest.
The devices are a block of a 4x4x8 slice.
Arguments:
- x_in: bfloat16 [16, 4, 128, 768], P(('dp', 'pp')), parts along dimension 0
- dy_out: bfloat16 [16, 4, 128, 768], P(('dp', 'pp')), parts along dimension 0
- w_qkv: bfloat16 [8, 2, 1, 768, 3, 16, 48], P('pp')
- w_attn: bfloat16 [8, 2, 1, 16, 48, 768], P('pp')
- w_fc: bfloat16 [8, 2, 1, 768, 3072], P('pp')
- w_proj: bfloat16 [8, 2, 1, 3072, 768], P('pp')
- b_qkv: bfloat16 [8, 2, 1, 3, 16, 48], P('pp')
- b_fc: bfloat16 [8, 2, 1, 3072], P('pp')
- vec_d: bfloat16 [8, 2, 1, 6, 768], P('pp')
Outputs:
- output 1: bfloat16 [16, 4, 128, 768], P(('dp', 'pp')), parts along dimension 0
- output 2: bfloat16 [16, 4, 128, 768], P(('dp', 'pp')), parts along dimension 0
- output 3: float32 [16, 2, 1, 768, 3, 16, 48], P(('dp', 'pp')), parts along dimension 0
- output 4: float32 [16, 2, 1, 16, 48, 768], P(('dp', 'pp')), parts along dimension 0
- output 5: float32 [16, 2, 1, 768, 3072], P(('dp', 'pp')), parts along dimension 0
- output 6: float32 [16, 2, 1, 3072, 768], P(('dp', 'pp')), parts along dimension 0
- output 7: float32 [16, 2, 1, 3, 16, 48], P(('dp', 'pp')), parts along dimension 0
- output 8: float32 [16, 2, 1, 3072], P(('dp', 'pp')), parts along dimension 0
- output 9: float32 [16, 2, 1, 6, 768], P(('dp', 'pp')), parts along dimension 0
There are 2 independent parts. A program takes and returns all parts, laid end to end along the dimension named above; an argument that names none is the same for every part.
All inputs are finite; a program needn't handle non-finite values.
Results may differ from a plain program's by a relative error of at most 0.02.
Values are sent between devices in bfloat16 or wider.
A program may use at most 768 MiB of HBM per device.

v0:
```python
import jax
import jax.numpy as jnp
from jax import lax
from jax.sharding import PartitionSpec as P

EPSILON = 1e-5


def layer_norm(rows_in, ln_gain, ln_shift):
    rows_f32 = rows_in.astype(jnp.float32)
    row_mean = jnp.mean(rows_f32, axis=-1, keepdims=True)
    centered = rows_f32 - row_mean
    row_var = jnp.mean(centered * centered, axis=-1, keepdims=True)
    scaled = centered * lax.rsqrt(row_var + EPSILON)
    return (scaled * ln_gain.astype(jnp.float32) + ln_shift.astype(jnp.float32)).astype(jnp.bfloat16)


def gpt_layer(hidden_in, layer_w):
    w_qkv, w_attn, w_fc, w_proj, b_qkv, b_fc, vec_d = layer_w
    n_batch, seq_len, d_model = hidden_in.shape
    n_heads, head_dim = w_qkv.shape[-2], w_qkv.shape[-1]
    tokens = n_batch * seq_len
    flat_rows = hidden_in.reshape(tokens, d_model)
    normed = layer_norm(flat_rows, vec_d[0], vec_d[1])
    qkv_proj = jnp.dot(normed, w_qkv.reshape(d_model, 3 * d_model), preferred_element_type=jnp.float32)
    qkv_proj = (qkv_proj + b_qkv.reshape(3 * d_model).astype(jnp.float32)).astype(jnp.bfloat16)
    qkv_proj = qkv_proj.reshape(n_batch, seq_len, 3, n_heads, head_dim)
    query_heads = qkv_proj[:, :, 0]
    key_heads = qkv_proj[:, :, 1]
    value_heads = qkv_proj[:, :, 2]
    scores = jnp.einsum('bqhe,bkhe->bhqk', query_heads, key_heads, preferred_element_type=jnp.float32) * (head_dim ** -0.5)
    causal = lax.broadcasted_iota(jnp.int32, (seq_len, seq_len), 0) >= lax.broadcasted_iota(jnp.int32, (seq_len, seq_len), 1)
    scores = jnp.where(causal, scores, -1e30)
    attn_probs = jax.nn.softmax(scores, axis=-1).astype(jnp.bfloat16)
    mixed_heads = jnp.einsum('bhqk,bkhe->bqhe', attn_probs, value_heads, preferred_element_type=jnp.float32).astype(jnp.bfloat16)
    attn_out = jnp.dot(mixed_heads.reshape(tokens, d_model), w_attn.reshape(d_model, d_model), preferred_element_type=jnp.float32)
    residual = (flat_rows.astype(jnp.float32) + attn_out + vec_d[2].astype(jnp.float32)).astype(jnp.bfloat16)
    normed_two = layer_norm(residual, vec_d[3], vec_d[4])
    hidden = jnp.dot(normed_two, w_fc, preferred_element_type=jnp.float32) + b_fc.astype(jnp.float32)
    hidden = jax.nn.gelu(hidden, approximate=True).astype(jnp.bfloat16)
    mlp_out = jnp.dot(hidden, w_proj, preferred_element_type=jnp.float32) + vec_d[5].astype(jnp.float32)
    return (residual.astype(jnp.float32) + mlp_out).astype(jnp.bfloat16).reshape(n_batch, seq_len, d_model)


def stage_forward(hidden_in, stage_w):
    for layer_idx in range(stage_w[0].shape[0]):
        hidden_in = gpt_layer(hidden_in, tuple(t[layer_idx] for t in stage_w))
    return hidden_in


def skip_forward(hidden_in, stage_w):
    return jnp.zeros_like(hidden_in)


def stage_backward(hidden_in, cotangent, stage_w, grad_acc):
    _, pull_back = jax.vjp(stage_forward, hidden_in, stage_w)
    d_input, d_weights = pull_back(cotangent)
    return d_input, tuple(a + g.astype(jnp.float32) for a, g in zip(grad_acc, d_weights))


def skip_backward(hidden_in, cotangent, stage_w, grad_acc):
    return jnp.zeros_like(hidden_in), grad_acc


def pick_row(buffer, index):
    return lax.dynamic_index_in_dim(buffer, index, 0, keepdims=False)


def store_row(buffer, row_val, index):
    return lax.dynamic_update_index_in_dim(buffer, row_val, index, 0)


def solution(mesh):
    n_stages = mesh.shape['pp']
    last = n_stages - 1
    to_next = [(i, i + 1) for i in range(last)]
    to_prev = [(i + 1, i) for i in range(last)]
    opposite = [(i, last - i) for i in range(n_stages)]
    data_spec = P(('dp', 'pp'))
    weight_spec = P('pp')

    def per_device(x_loc, dy_loc, *weights):
        dev_pos = lax.axis_index('pp')
        down_w = tuple(t[0, 0] for t in weights)
        up_w = tuple(t[0, 1] for t in weights)
        x_all = lax.all_gather(x_loc, 'pp', tiled=True)
        dy_all = lax.all_gather(dy_loc, 'pp', tiled=True)
        n_micro = x_all.shape[0]
        half_micro = n_micro // 2
        n_steps = half_micro + last
        act_shape = x_loc.shape[1:]
        zero_act = jnp.zeros(act_shape, x_loc.dtype)
        stash_zero = jnp.zeros((half_micro + 1,) + act_shape, x_loc.dtype)
        out_zero = jnp.zeros((n_micro + 1,) + act_shape, x_loc.dtype)

        def forward_step(step, carry):
            down_in, up_in, down_stash, up_stash, y_buf = carry
            down_idx = step - dev_pos
            up_idx = step - (last - dev_pos)
            down_ok = (down_idx >= 0) & (down_idx < half_micro)
            up_ok = (up_idx >= 0) & (up_idx < half_micro)
            down_row = jnp.clip(down_idx, 0, half_micro - 1)
            up_row = jnp.clip(up_idx, 0, half_micro - 1)
            down_act = jnp.where(dev_pos == 0, pick_row(x_all, down_row), down_in)
            up_act = jnp.where(dev_pos == last, pick_row(x_all, half_micro + up_row), up_in)
            down_stash = store_row(down_stash, down_act, jnp.where(down_ok, down_idx, half_micro))
            up_stash = store_row(up_stash, up_act, jnp.where(up_ok, up_idx, half_micro))
            down_out = lax.cond(down_ok, stage_forward, skip_forward, down_act, down_w)
            up_out = lax.cond(up_ok, stage_forward, skip_forward, up_act, up_w)
            y_buf = store_row(y_buf, down_out, jnp.where(down_ok & (dev_pos == last), down_idx, n_micro))
            y_buf = store_row(y_buf, up_out, jnp.where(up_ok & (dev_pos == 0), half_micro + up_idx, n_micro))
            down_in = lax.ppermute(down_out, 'pp', to_next)
            up_in = lax.ppermute(up_out, 'pp', to_prev)
            return down_in, up_in, down_stash, up_stash, y_buf

        fwd_init = (zero_act, zero_act, stash_zero, stash_zero, out_zero)
        _, _, down_stash, up_stash, y_buf = lax.fori_loop(0, n_steps, forward_step, fwd_init)
        y_loc = lax.psum_scatter(y_buf[:n_micro], 'pp', scatter_dimension=0, tiled=True)
        grad_zero = tuple(jnp.zeros(t.shape, jnp.float32) for t in down_w)

        def backward_step(step, carry):
            down_cot_in, up_cot_in, down_acc, up_acc, dx_buf = carry
            down_idx = step - (last - dev_pos)
            up_idx = step - dev_pos
            down_ok = (down_idx >= 0) & (down_idx < half_micro)
            up_ok = (up_idx >= 0) & (up_idx < half_micro)
            down_row = jnp.clip(down_idx, 0, half_micro - 1)
            up_row = jnp.clip(up_idx, 0, half_micro - 1)
            down_cot = jnp.where(dev_pos == last, pick_row(dy_all, down_row), down_cot_in)
            up_cot = jnp.where(dev_pos == 0, pick_row(dy_all, half_micro + up_row), up_cot_in)
            down_dx, down_acc = lax.cond(down_ok, stage_backward, skip_backward, pick_row(down_stash, down_row), down_cot, down_w, down_acc)
            up_dx, up_acc = lax.cond(up_ok, stage_backward, skip_backward, pick_row(up_stash, up_row), up_cot, up_w, up_acc)
            dx_buf = store_row(dx_buf, down_dx, jnp.where(down_ok & (dev_pos == 0), down_idx, n_micro))
            dx_buf = store_row(dx_buf, up_dx, jnp.where(up_ok & (dev_pos == last), half_micro + up_idx, n_micro))
            down_cot_in = lax.ppermute(down_dx, 'pp', to_prev)
            up_cot_in = lax.ppermute(up_dx, 'pp', to_next)
            return down_cot_in, up_cot_in, down_acc, up_acc, dx_buf

        bwd_init = (zero_act, zero_act, grad_zero, grad_zero, out_zero)
        _, _, down_acc, up_acc, dx_buf = lax.fori_loop(0, n_steps, backward_step, bwd_init)
        dx_loc = lax.psum_scatter(dx_buf[:n_micro], 'pp', scatter_dimension=0, tiled=True)
        peer_down = tuple(lax.ppermute(g, 'pp', opposite) for g in down_acc)
        peer_up = tuple(lax.ppermute(g, 'pp', opposite) for g in up_acc)
        grads = tuple(jnp.stack([mine_d + peer_u, mine_u + peer_d], axis=0)[None] for mine_d, mine_u, peer_d, peer_u in zip(down_acc, up_acc, peer_down, peer_up))
        return (y_loc, dx_loc) + grads

    return jax.shard_map(per_device, mesh=mesh, in_specs=(data_spec, data_spec) + (weight_spec,) * 7, out_specs=(data_spec, data_spec) + (data_spec,) * 7, check_vma=False)
```

profile of v0, /device:TPU:127, one launch (start us, length us, event | category | flops | bytes accessed | tf_op | source)
XLA Modules:
  0.0 4199.4 jit_solution(11489457124973538848)
XLA Ops:
  55.2 664.5 %while.70 = (s32[]{:T(128)}, bf16[4,128,768]{2,1,0:T(8,128)(2,1)}, bf16[4,128,768]{2,1,0:T(8,128)(2,1)S(1)}, bf16[5,4,128,768]{3,2,1,0:T(8,128)(2,1)}, bf16[5,4,...) while((s32[]{:T(128)}, bf16[4,128,768]{2,1,0:T(8,128)(2,1)}, ...), condition=%wide.region_17.18_spmd, body=%wide.region_0.17_spmd.sunk | while | flops 14977909760 | bytes 224343248 | solution.py:117
  351.1 127.2 %collective-permute-start.1 = (bf16[4,128,768]{2,1,0:T(8,128)(2,1)}, bf16[4,128,768]{2,1,0:T(8,128)(2,1)S(1)}, u32[]{:S(2)}, u32[]{:S(2)}) collective-permute-start(bf16[4,128,768]{2,1,0:T(8,128)(2,1)} %get-tuple-element.2613), channel_id=1, source_target_pairs={{1,0},{2,1},{3,2},{4,3},{5,4},{6,5},{7,6},{9,8},{10,9},{11,10},{12... | collective-permute-start | bytes 2359304 | tf_op jit(solution)/shard_map/while/body/eval_jaxpr/ppermute | solution.py:113
  763.1 2138.2 %while.71 = (s32[]{:T(128)}, bf16[4,128,768]{2,1,0:T(8,128)(2,1)}, bf16[4,128,768]{2,1,0:T(8,128)(2,1)}, f32[1,768,3,16,48]{1,4,3,2,0:T(8,128)}, f32[1,16,48,768...) while((s32[]{:T(128)}, bf16[4,128,768]{2,1,0:T(8,128)(2,1)}, ...), condition=%wide.region_62.63_spmd, body=%wide.region_19.62_spmd.sunk | while | flops 40152825856 | bytes 1154921856 | solution.py:140
  763.5 107.3 %conditional.10 = (bf16[4,128,768]{2,1,0:T(8,128)(2,1)}, f32[1,768,3,16,48]{1,4,3,2,0:T(8,128)}, f32[1,16,48,768]{3,2,1,0:T(8,128)}, f32[1,768,3072]{2,1,0:T(8,1...) conditional(s32[]{:T(128)} %convert_element_type.1796, ...), branch_computations={%region_20.20_spmd, %region_21.40_spmd} | conditional | flops 20076412928 | bytes 568662144 | solution.py:131
  886.9 107.3 %conditional.10 = (bf16[4,128,768]{2,1,0:T(8,128)(2,1)}, f32[1,768,3,16,48]{1,4,3,2,0:T(8,128)}, f32[1,16,48,768]{3,2,1,0:T(8,128)}, f32[1,768,3072]{2,1,0:T(8,1...) conditional(s32[]{:T(128)} %convert_element_type.1796, ...), branch_computations={%region_20.20_spmd, %region_21.40_spmd} | conditional | flops 20076412928 | bytes 568662144 | solution.py:131
  1010.2 107.3 %conditional.10 = (bf16[4,128,768]{2,1,0:T(8,128)(2,1)}, f32[1,768,3,16,48]{1,4,3,2,0:T(8,128)}, f32[1,16,48,768]{3,2,1,0:T(8,128)}, f32[1,768,3072]{2,1,0:T(8,1...) conditional(s32[]{:T(128)} %convert_element_type.1796, ...), branch_computations={%region_20.20_spmd, %region_21.40_spmd} | conditional | flops 20076412928 | bytes 568662144 | solution.py:131
  1142.0 107.3 %conditional.10 = (bf16[4,128,768]{2,1,0:T(8,128)(2,1)}, f32[1,768,3,16,48]{1,4,3,2,0:T(8,128)}, f32[1,16,48,768]{3,2,1,0:T(8,128)}, f32[1,768,3072]{2,1,0:T(8,1...) conditional(s32[]{:T(128)} %convert_element_type.1796, ...), branch_computations={%region_20.20_spmd, %region_21.40_spmd} | conditional | flops 20076412928 | bytes 568662144 | solution.py:131
  1284.5 110.2 %collective-permute-start.2 = (bf16[4,128,768]{2,1,0:T(8,128)(2,1)}, bf16[4,128,768]{2,1,0:T(8,128)(2,1)}, u32[]{:S(2)}, u32[]{:S(2)}) collective-permute-start(bf16[4,128,768]{2,1,0:T(8,128)(2,1)} %get-tuple-element.2657), channel_id=1, source_target_pairs={{1,0},{2,1},{3,2},{4,3},{5,4},{6,5},{7,6},{9,8},{10,9},{11,10},{12... | collective-permute-start | bytes 2359304 | tf_op jit(solution)/shard_map/while/body/eval_jaxpr/ppermute | solution.py:135
  1407.7 156.1 %collective-permute-start.2 = (bf16[4,128,768]{2,1,0:T(8,128)(2,1)}, bf16[4,128,768]{2,1,0:T(8,128)(2,1)}, u32[]{:S(2)}, u32[]{:S(2)}) collective-permute-start(bf16[4,128,768]{2,1,0:T(8,128)(2,1)} %get-tuple-element.2657), channel_id=1, source_target_pairs={{1,0},{2,1},{3,2},{4,3},{5,4},{6,5},{7,6},{9,8},{10,9},{11,10},{12... | collective-permute-start | bytes 2359304 | tf_op jit(solution)/shard_map/while/body/eval_jaxpr/ppermute | solution.py:135
  1571.3 213.6 %collective-permute-done.3 = bf16[4,128,768]{2,1,0:T(8,128)(2,1)S(1)} collective-permute-done((bf16[4,128,768]{2,1,0:T(8,128)(2,1)}, bf16[4,128,768]{2,1,0:T(8,128)(2,1)S(1)}, u32[]{:S(2)}, u32[]{:S(2)}) %collective-permute-start.3) | collective-permute-done | bytes 786464 | tf_op jit(solution)/shard_map/while/body/eval_jaxpr/ppermute | solution.py:136
  1787.7 145.6 %collective-permute-start.2 = (bf16[4,128,768]{2,1,0:T(8,128)(2,1)}, bf16[4,128,768]{2,1,0:T(8,128)(2,1)}, u32[]{:S(2)}, u32[]{:S(2)}) collective-permute-start(bf16[4,128,768]{2,1,0:T(8,128)(2,1)} %get-tuple-element.2657), channel_id=1, source_target_pairs={{1,0},{2,1},{3,2},{4,3},{5,4},{6,5},{7,6},{9,8},{10,9},{11,10},{12... | collective-permute-start | bytes 2359304 | tf_op jit(solution)/shard_map/while/body/eval_jaxpr/ppermute | solution.py:135
  1940.7 131.9 %collective-permute-done.3 = bf16[4,128,768]{2,1,0:T(8,128)(2,1)S(1)} collective-permute-done((bf16[4,128,768]{2,1,0:T(8,128)(2,1)}, bf16[4,128,768]{2,1,0:T(8,128)(2,1)S(1)}, u32[]{:S(2)}, u32[]{:S(2)}) %collective-permute-start.3) | collective-permute-done | bytes 786464 | tf_op jit(solution)/shard_map/while/body/eval_jaxpr/ppermute | solution.py:136
  2075.4 119.9 %collective-permute-start.2 = (bf16[4,128,768]{2,1,0:T(8,128)(2,1)}, bf16[4,128,768]{2,1,0:T(8,128)(2,1)}, u32[]{:S(2)}, u32[]{:S(2)}) collective-permute-start(bf16[4,128,768]{2,1,0:T(8,128)(2,1)} %get-tuple-element.2657), channel_id=1, source_target_pairs={{1,0},{2,1},{3,2},{4,3},{5,4},{6,5},{7,6},{9,8},{10,9},{11,10},{12... | collective-permute-start | bytes 2359304 | tf_op jit(solution)/shard_map/while/body/eval_jaxpr/ppermute | solution.py:135
  2195.2 128.4 %conditional.11 = (bf16[4,128,768]{2,1,0:T(8,128)(2,1)}, f32[1,768,3,16,48]{1,4,3,2,0:T(8,128)}, f32[1,16,48,768]{3,2,1,0:T(8,128)}, f32[1,768,3072]{2,1,0:T(8,1...) conditional(s32[]{:T(128)} %convert_element_type.1797, ...), branch_computations={%region_41.41_spmd, %region_42.61_spmd} | conditional | flops 20076412928 | bytes 573528448 | solution.py:132
  2350.7 128.3 %conditional.11 = (bf16[4,128,768]{2,1,0:T(8,128)(2,1)}, f32[1,768,3,16,48]{1,4,3,2,0:T(8,128)}, f32[1,16,48,768]{3,2,1,0:T(8,128)}, f32[1,768,3072]{2,1,0:T(8,1...) conditional(s32[]{:T(128)} %convert_element_type.1797, ...), branch_computations={%region_41.41_spmd, %region_42.61_spmd} | conditional | flops 20076412928 | bytes 573528448 | solution.py:132
  2484.6 86.4 %collective-permute-done.3 = bf16[4,128,768]{2,1,0:T(8,128)(2,1)S(1)} collective-permute-done((bf16[4,128,768]{2,1,0:T(8,128)(2,1)}, bf16[4,128,768]{2,1,0:T(8,128)(2,1)S(1)}, u32[]{:S(2)}, u32[]{:S(2)}) %collective-permute-start.3) | collective-permute-done | bytes 786464 | tf_op jit(solution)/shard_map/while/body/eval_jaxpr/ppermute | solution.py:136
  2603.1 128.3 %conditional.11 = (bf16[4,128,768]{2,1,0:T(8,128)(2,1)}, f32[1,768,3,16,48]{1,4,3,2,0:T(8,128)}, f32[1,16,48,768]{3,2,1,0:T(8,128)}, f32[1,768,3072]{2,1,0:T(8,1...) conditional(s32[]{:T(128)} %convert_element_type.1797, ...), branch_computations={%region_41.41_spmd, %region_42.61_spmd} | conditional | flops 20076412928 | bytes 573528448 | solution.py:132
  2758.6 128.3 %conditional.11 = (bf16[4,128,768]{2,1,0:T(8,128)(2,1)}, f32[1,768,3,16,48]{1,4,3,2,0:T(8,128)}, f32[1,16,48,768]{3,2,1,0:T(8,128)}, f32[1,768,3072]{2,1,0:T(8,1...) conditional(s32[]{:T(128)} %convert_element_type.1797, ...), branch_computations={%region_41.41_spmd, %region_42.61_spmd} | conditional | flops 20076412928 | bytes 573528448 | solution.py:132
  2908.1 402.4 %collective-permute-done.13 = f32[1,3,16,48]{3,2,1,0:T(8,128)S(1)} collective-permute-done((f32[1,3,16,48]{3,2,1,0:T(8,128)S(1)}, f32[1,3,16,48]{3,2,1,0:T(8,128)S(1)}, u32[]{:S(2)}, u32[]{:S(2)}) %collective-permute-start.13) | collective-permute-done | bytes 9248 | tf_op jit(solution)/shard_map/ppermute | solution.py:142
  3318.6 153.1 %collective-permute-done.14 = f32[1,3072]{1,0:T(1,128)S(1)} collective-permute-done((f32[1,3072]{1,0:T(1,128)}, f32[1,3072]{1,0:T(1,128)S(1)}, u32[]{:S(2)}, u32[]{:S(2)}) %collective-permute-start.14) | collective-permute-done | bytes 12320 | tf_op jit(solution)/shard_map/ppermute | solution.py:143
  3479.1 52.2 %collective-permute-done.6 = f32[1,16,48,768]{3,2,1,0:T(8,128)} collective-permute-done((f32[1,16,48,768]{3,2,1,0:T(8,128)}, f32[1,16,48,768]{3,2,1,0:T(8,128)}, u32[]{:S(2)}, u32[]{:S(2)}) %collective-permute-start.6) | collective-permute-done | bytes 2359328 | tf_op jit(solution)/shard_map/ppermute | solution.py:143
  3591.4 171.5 %collective-permute-done.8 = f32[1,768,3072]{2,1,0:T(8,128)} collective-permute-done((f32[1,768,3072]{2,1,0:T(8,128)}, f32[1,768,3072]{2,1,0:T(8,128)}, u32[]{:S(2)}, u32[]{:S(2)}) %collective-permute-start.8) | collective-permute-done | bytes 9437216 | tf_op jit(solution)/shard_map/ppermute | solution.py:143
  3789.1 176.1 %collective-permute-done.11 = f32[1,3072,768]{2,1,0:T(8,128)} collective-permute-done((f32[1,3072,768]{2,1,0:T(8,128)}, f32[1,3072,768]{2,1,0:T(8,128)}, u32[]{:S(2)}, u32[]{:S(2)}) %collective-permute-start.11) | collective-permute-done | bytes 9437216 | tf_op jit(solution)/shard_map/ppermute | solution.py:142
  3976.3 190.5 %collective-permute-done.10 = f32[1,3072,768]{2,1,0:T(8,128)} collective-permute-done((f32[1,3072,768]{2,1,0:T(8,128)}, f32[1,3072,768]{2,1,0:T(8,128)}, u32[]{:S(2)}, u32[]{:S(2)}) %collective-permute-start.10) | collective-permute-done | bytes 9437216 | tf_op jit(solution)/shard_map/ppermute | solution.py:143
  (1886 shorter events, 2219.4 us)
Async XLA Ops:
  8.0 717.9 %all-gather.5.cloned.1.call-start = ((), (), s32[]{:S(2)}) async-start(), calls=%async_computation.4 | async-start | bytes 7077888 | tf_op jit(solution)/shard_map/all_gather | solution.py:87
  8.8 4183.8 %reduce-scatter.3.cloned.1.call-start = ((), (), s32[]{:S(2)}) async-start(), calls=%async_computation.3 | async-start | bytes 7077888 | tf_op jit(solution)/shard_map/reduce_scatter | solution.py:118
  347.9 134.6 %collective-permute-start = (bf16[4,128,768]{2,1,0:T(8,128)(2,1)}, bf16[4,128,768]{2,1,0:T(8,128)(2,1)}, u32[]{:S(2)}, u32[]{:S(2)}) collective-permute-start(bf16[4,128,768]{2,1,0:T(8,128)(2,1)} %get-tuple-element.2611), channel_id=1, source_target_pairs={{0,1},{1,2},{2,3},{3,4},{4,5},{5,6},{6,7},{8,9},{9,10},{10,11},{11... | collective-permute-start | bytes 2359304 | tf_op jit(solution)/shard_map/while/body/eval_jaxpr/ppermute | solution.py:112
  351.1 131.4 %collective-permute-start.1 = (bf16[4,128,768]{2,1,0:T(8,128)(2,1)}, bf16[4,128,768]{2,1,0:T(8,128)(2,1)S(1)}, u32[]{:S(2)}, u32[]{:S(2)}) collective-permute-start(bf16[4,128,768]{2,1,0:T(8,128)(2,1)} %get-tuple-element.2613), channel_id=1, source_target_pairs={{1,0},{2,1},{3,2},{4,3},{5,4},{6,5},{7,6},{9,8},{10,9},{11,10},{12... | collective-permute-start | bytes 2359304 | tf_op jit(solution)/shard_map/while/body/eval_jaxpr/ppermute | solution.py:113
  725.8 3466.8 %reduce-scatter.5.cloned.1.call-start = ((), (), s32[]{:S(2)}) async-start(), calls=%async_computation.5 | async-start | bytes 7077888 | tf_op jit(solution)/shard_map/reduce_scatter | solution.py:141
  1284.5 118.9 %collective-permute-start.2 = (bf16[4,128,768]{2,1,0:T(8,128)(2,1)}, bf16[4,128,768]{2,1,0:T(8,128)(2,1)}, u32[]{:S(2)}, u32[]{:S(2)}) collective-permute-start(bf16[4,128,768]{2,1,0:T(8,128)(2,1)} %get-tuple-element.2657), channel_id=1, source_target_pairs={{1,0},{2,1},{3,2},{4,3},{5,4},{6,5},{7,6},{9,8},{10,9},{11,10},{12... | collective-permute-start | bytes 2359304 | tf_op jit(solution)/shard_map/while/body/eval_jaxpr/ppermute | solution.py:135
  1407.7 163.5 %collective-permute-start.2 = (bf16[4,128,768]{2,1,0:T(8,128)(2,1)}, bf16[4,128,768]{2,1,0:T(8,128)(2,1)}, u32[]{:S(2)}, u32[]{:S(2)}) collective-permute-start(bf16[4,128,768]{2,1,0:T(8,128)(2,1)} %get-tuple-element.2657), channel_id=1, source_target_pairs={{1,0},{2,1},{3,2},{4,3},{5,4},{6,5},{7,6},{9,8},{10,9},{11,10},{12... | collective-permute-start | bytes 2359304 | tf_op jit(solution)/shard_map/while/body/eval_jaxpr/ppermute | solution.py:135
  1565.8 219.1 %collective-permute-start.3 = (bf16[4,128,768]{2,1,0:T(8,128)(2,1)}, bf16[4,128,768]{2,1,0:T(8,128)(2,1)S(1)}, u32[]{:S(2)}, u32[]{:S(2)}) collective-permute-start(bf16[4,128,768]{2,1,0:T(8,128)(2,1)} %get-tuple-element.2658), channel_id=1, source_target_pairs={{0,1},{1,2},{2,3},{3,4},{4,5},{5,6},{6,7},{8,9},{9,10},{10,11},{11... | collective-permute-start | bytes 2359304 | tf_op jit(solution)/shard_map/while/body/eval_jaxpr/ppermute | solution.py:136
  1787.7 153.0 %collective-permute-start.2 = (bf16[4,128,768]{2,1,0:T(8,128)(2,1)}, bf16[4,128,768]{2,1,0:T(8,128)(2,1)}, u32[]{:S(2)}, u32[]{:S(2)}) collective-permute-start(bf16[4,128,768]{2,1,0:T(8,128)(2,1)} %get-tuple-element.2657), channel_id=1, source_target_pairs={{1,0},{2,1},{3,2},{4,3},{5,4},{6,5},{7,6},{9,8},{10,9},{11,10},{12... | collective-permute-start | bytes 2359304 | tf_op jit(solution)/shard_map/while/body/eval_jaxpr/ppermute | solution.py:135
  1935.2 137.4 %collective-permute-start.3 = (bf16[4,128,768]{2,1,0:T(8,128)(2,1)}, bf16[4,128,768]{2,1,0:T(8,128)(2,1)S(1)}, u32[]{:S(2)}, u32[]{:S(2)}) collective-permute-start(bf16[4,128,768]{2,1,0:T(8,128)(2,1)} %get-tuple-element.2658), channel_id=1, source_target_pairs={{0,1},{1,2},{2,3},{3,4},{4,5},{5,6},{6,7},{8,9},{9,10},{10,11},{11... | collective-permute-start | bytes 2359304 | tf_op jit(solution)/shard_map/while/body/eval_jaxpr/ppermute | solution.py:136
  2075.4 253.8 %collective-permute-start.2 = (bf16[4,128,768]{2,1,0:T(8,128)(2,1)}, bf16[4,128,768]{2,1,0:T(8,128)(2,1)}, u32[]{:S(2)}, u32[]{:S(2)}) collective-permute-start(bf16[4,128,768]{2,1,0:T(8,128)(2,1)} %get-tuple-element.2657), channel_id=1, source_target_pairs={{1,0},{2,1},{3,2},{4,3},{5,4},{6,5},{7,6},{9,8},{10,9},{11,10},{12... | collective-permute-start | bytes 2359304 | tf_op jit(solution)/shard_map/while/body/eval_jaxpr/ppermute | solution.py:135
  2340.9 143.6 %collective-permute-start.2 = (bf16[4,128,768]{2,1,0:T(8,128)(2,1)}, bf16[4,128,768]{2,1,0:T(8,128)(2,1)}, u32[]{:S(2)}, u32[]{:S(2)}) collective-permute-start(bf16[4,128,768]{2,1,0:T(8,128)(2,1)} %get-tuple-element.2657), channel_id=1, source_target_pairs={{1,0},{2,1},{3,2},{4,3},{5,4},{6,5},{7,6},{9,8},{10,9},{11,10},{12... | collective-permute-start | bytes 2359304 | tf_op jit(solution)/shard_map/while/body/eval_jaxpr/ppermute | solution.py:135
  2582.8 154.2 %collective-permute-start.2 = (bf16[4,128,768]{2,1,0:T(8,128)(2,1)}, bf16[4,128,768]{2,1,0:T(8,128)(2,1)}, u32[]{:S(2)}, u32[]{:S(2)}) collective-permute-start(bf16[4,128,768]{2,1,0:T(8,128)(2,1)} %get-tuple-element.2657), channel_id=1, source_target_pairs={{1,0},{2,1},{3,2},{4,3},{5,4},{6,5},{7,6},{9,8},{10,9},{11,10},{12... | collective-permute-start | bytes 2359304 | tf_op jit(solution)/shard_map/while/body/eval_jaxpr/ppermute | solution.py:135
  2748.8 143.6 %collective-permute-start.2 = (bf16[4,128,768]{2,1,0:T(8,128)(2,1)}, bf16[4,128,768]{2,1,0:T(8,128)(2,1)}, u32[]{:S(2)}, u32[]{:S(2)}) collective-permute-start(bf16[4,128,768]{2,1,0:T(8,128)(2,1)} %get-tuple-element.2657), channel_id=1, source_target_pairs={{1,0},{2,1},{3,2},{4,3},{5,4},{6,5},{7,6},{9,8},{10,9},{11,10},{12... | collective-permute-start | bytes 2359304 | tf_op jit(solution)/shard_map/while/body/eval_jaxpr/ppermute | solution.py:135
  2901.3 638.5 %collective-permute-start.5 = (f32[1,768,3,16,48]{1,4,3,2,0:T(8,128)}, f32[1,768,3,16,48]{1,4,3,2,0:T(8,128)}, u32[]{:S(2)}, u32[]{:S(2)}) collective-permute-start(f32[1,768,3,16,48]{1,4,3,2,0:T(8,128)} %get-tuple-element.1965), channel_id=1, source_target_pairs={{0,7},{1,6},{2,5},{3,4},{4,3},{5,2},{6,1},{7,0},{8,15},{9,14},{10,... | collective-permute-start | bytes 21233672 | tf_op jit(solution)/shard_map/ppermute | solution.py:142
  2901.4 575.7 %collective-permute-start.7 = (f32[1,16,48,768]{3,2,1,0:T(8,128)}, f32[1,16,48,768]{3,2,1,0:T(8,128)}, u32[]{:S(2)}, u32[]{:S(2)}) collective-permute-start(f32[1,16,48,768]{3,2,1,0:T(8,128)} %get-tuple-element.1967), channel_id=1, source_target_pairs={{0,7},{1,6},{2,5},{3,4},{4,3},{5,2},{6,1},{7,0},{8,15},{9,14},{10,... | collective-permute-start | bytes 7077896 | tf_op jit(solution)/shard_map/ppermute | solution.py:142
  2904.3 674.4 %collective-permute-start.9 = (f32[1,768,3072]{2,1,0:T(8,128)}, f32[1,768,3072]{2,1,0:T(8,128)}, u32[]{:S(2)}, u32[]{:S(2)}) collective-permute-start(f32[1,768,3072]{2,1,0:T(8,128)} %get-tuple-element.1969), channel_id=1, source_target_pairs={{0,7},{1,6},{2,5},{3,4},{4,3},{5,2},{6,1},{7,0},{8,15},{9,14},{10,... | collective-permute-start | bytes 28311560 | tf_op jit(solution)/shard_map/ppermute | solution.py:142
  2904.4 406.1 %collective-permute-start.13 = (f32[1,3,16,48]{3,2,1,0:T(8,128)S(1)}, f32[1,3,16,48]{3,2,1,0:T(8,128)S(1)}, u32[]{:S(2)}, u32[]{:S(2)}) collective-permute-start(f32[1,3,16,48]{3,2,1,0:T(8,128)S(1)} %get-tuple-element.1973), channel_id=1, source_target_pairs={{0,7},{1,6},{2,5},{3,4},{4,3},{5,2},{6,1},{7,0},{8,15},{9,14},{10,... | collective-permute-start | bytes 27656 | tf_op jit(solution)/shard_map/ppermute | solution.py:142
  2907.2 403.6 %collective-permute-start.12 = (f32[1,3,16,48]{3,2,1,0:T(8,128)}, f32[1,3,16,48]{3,2,1,0:T(8,128)S(1)}, u32[]{:S(2)}, u32[]{:S(2)}) collective-permute-start(f32[1,3,16,48]{3,2,1,0:T(8,128)} %get-tuple-element.1974), channel_id=1, source_target_pairs={{0,7},{1,6},{2,5},{3,4},{4,3},{5,2},{6,1},{7,0},{8,15},{9,14},{10,... | collective-permute-start | bytes 27656 | tf_op jit(solution)/shard_map/ppermute | solution.py:143
  3315.6 244.1 %collective-permute-start.4 = (f32[1,768,3,16,48]{1,4,3,2,0:T(8,128)}, f32[1,768,3,16,48]{1,4,3,2,0:T(8,128)}, u32[]{:S(2)}, u32[]{:S(2)}) collective-permute-start(f32[1,768,3,16,48]{1,4,3,2,0:T(8,128)} %get-tuple-element.1966), channel_id=1, source_target_pairs={{0,7},{1,6},{2,5},{3,4},{4,3},{5,2},{6,1},{7,0},{8,15},{9,14},{10,... | collective-permute-start | bytes 21233672 | tf_op jit(solution)/shard_map/ppermute | solution.py:143
  3317.8 153.9 %collective-permute-start.14 = (f32[1,3072]{1,0:T(1,128)}, f32[1,3072]{1,0:T(1,128)S(1)}, u32[]{:S(2)}, u32[]{:S(2)}) collective-permute-start(f32[1,3072]{1,0:T(1,128)} %get-tuple-element.1976), channel_id=1, source_target_pairs={{0,7},{1,6},{2,5},{3,4},{4,3},{5,2},{6,1},{7,0},{8,15},{9,14},{10,... | collective-permute-start | bytes 36872 | tf_op jit(solution)/shard_map/ppermute | solution.py:143
  3477.1 285.9 %collective-permute-start.8 = (f32[1,768,3072]{2,1,0:T(8,128)}, f32[1,768,3072]{2,1,0:T(8,128)}, u32[]{:S(2)}, u32[]{:S(2)}) collective-permute-start(f32[1,768,3072]{2,1,0:T(8,128)} %get-tuple-element.1970), channel_id=1, source_target_pairs={{0,7},{1,6},{2,5},{3,4},{4,3},{5,2},{6,1},{7,0},{8,15},{9,14},{10,... | collective-permute-start | bytes 28311560 | tf_op jit(solution)/shard_map/ppermute | solution.py:143
  3531.3 434.0 %collective-permute-start.11 = (f32[1,3072,768]{2,1,0:T(8,128)}, f32[1,3072,768]{2,1,0:T(8,128)}, u32[]{:S(2)}, u32[]{:S(2)}) collective-permute-start(f32[1,3072,768]{2,1,0:T(8,128)} %get-tuple-element.1971), channel_id=1, source_target_pairs={{0,7},{1,6},{2,5},{3,4},{4,3},{5,2},{6,1},{7,0},{8,15},{9,14},{10,... | collective-permute-start | bytes 28311560 | tf_op jit(solution)/shard_map/ppermute | solution.py:142
  3539.7 627.1 %collective-permute-start.10 = (f32[1,3072,768]{2,1,0:T(8,128)}, f32[1,3072,768]{2,1,0:T(8,128)}, u32[]{:S(2)}, u32[]{:S(2)}) collective-permute-start(f32[1,3072,768]{2,1,0:T(8,128)} %get-tuple-element.1972), channel_id=1, source_target_pairs={{0,7},{1,6},{2,5},{3,4},{4,3},{5,2},{6,1},{7,0},{8,15},{9,14},{10,... | collective-permute-start | bytes 28311560 | tf_op jit(solution)/shard_map/ppermute | solution.py:143
  (446 other events, 4813.4 us)
Sparse Core Ops, SparseCore 0:
  9.6 36.1 all-gather.2
  47.4 36.6 all-gather.4
  725.9 93.0 reduce-scatter.2
  3537.6 98.2 reduce-scatter.4
where the time goes:
time: 4220 us; the launch traced here: 4200 us
  waiting for transfers between devices  1600 us (38%)
  starting transfers between devices  918 us (22%)
  matrix products  594 us (14%)
  local copies, waits for them, and re-layouts  586 us (14%)
  other arithmetic  402 us (10%)
  loops' own time  86 us (2%)
    ppermute x11, starting transfers between devices, backward_step(): down_cot_in = lax.ppermute(down_dx, 'pp', to_prev)  605 us
    ppermute x7, waiting for transfers between devices, per_device(): peer_down = tuple((lax.ppermute(g, 'pp', opposite) for g in down_acc))  584 us
    ppermute x7, waiting for transfers between devices, per_device(): peer_up = tuple((lax.ppermute(g, 'pp', opposite) for g in up_acc))  568 us
    ppermute x11, waiting for transfers between devices, backward_step(): up_cot_in = lax.ppermute(up_dx, 'pp', to_next)  436 us
    ppermute x11, starting transfers between devices, forward_step(): up_in = lax.ppermute(up_out, 'pp', to_prev)  265 us
    dot_general x24, matrix products, gpt_layer(): jnp.dot(hidden, w_proj, preferred_element_type=jnp.float32)  217 us
    dot_general x32, matrix products, gpt_layer(): jnp.dot(normed, w_qkv.reshape(d_model, 3 * d_model), preferred_element_ty...  136 us
    dot_general x32, matrix products, gpt_layer(): jnp.dot(normed_two, w_fc, preferred_element_type=jnp.float32)  116 us
  transfers between devices with their start and end apart: 62, of which 16 were waited for; matrix products, arithmetic and copies ran while one was open for 37% of the time, Pallas kernels for 0%

commit v1 on v0

v1 whole, which is shorter than its diff:
```python
import functools

import jax
import jax.numpy as jnp
from jax import lax
from jax.experimental import pallas as pl
from jax.experimental.pallas import tpu as pltpu
from jax.sharding import PartitionSpec as P

EPS = 1e-5
F32 = jnp.float32
BF16 = jnp.bfloat16
LANES = 128
ROWS = 96
CH = 256
SKEW = 3
K0 = 0.7978845608028654
K1 = K0 * 0.044715
VMEM_LIMIT = 67043328
HBM = pl.BlockSpec(memory_space=pl.ANY)


def dot(lhs, rhs, lc=1, rc=0):
    return lax.dot_general(lhs, rhs, (((lc,), (rc,)), ((), ())), preferred_element_type=F32)


def rows_sum(v):
    r, t = v.shape
    return jnp.sum(v.reshape(r // 8, 8, t), axis=0)


def wide(col, t):
    return jnp.concatenate([col] * (t // LANES), axis=1)


def lane_fold(v):
    return functools.reduce(jnp.add, [v[:, k:k + LANES] for k in range(0, v.shape[1], LANES)])


def block_diag(a, b):
    z = jnp.zeros_like(a)
    return jnp.concatenate([jnp.concatenate([a, z], 1), jnp.concatenate([z, b], 1)], 0)


def f_norm(src, gain, shift, dst, stats, row):
    d, t = src.shape
    acc = jnp.zeros((8, t), F32)
    for i in range(0, d, ROWS):
        acc += rows_sum(src[i:i + ROWS, :].astype(F32))
    mean = jnp.sum(acc, axis=0, keepdims=True) * (1.0 / d)
    acc = jnp.zeros((8, t), F32)
    for i in range(0, d, ROWS):
        c = src[i:i + ROWS, :].astype(F32) - mean
        acc += rows_sum(c * c)
    rstd = lax.rsqrt(jnp.sum(acc, axis=0, keepdims=True) * (1.0 / d) + EPS)
    for i in range(0, d, ROWS):
        c = (src[i:i + ROWS, :].astype(F32) - mean) * rstd
        g = wide(gain[i:i + ROWS, :].astype(F32), t)
        s = wide(shift[i:i + ROWS, :].astype(F32), t)
        dst[i:i + ROWS, :] = (c * g + s).astype(BF16)
    stats[row:row + 1, :] = mean
    stats[row + 1:row + 2, :] = rstd


def b_norm(dn, src, gain, skip, dst, stats, row, acc, lane):
    d, t = src.shape
    mean = stats[row:row + 1, :]
    rstd = stats[row + 1:row + 2, :]

    def terms(i):
        c = (src[i:i + ROWS, :].astype(F32) - mean) * rstd
        v = dn[i:i + ROWS, :].astype(F32)
        return c, v, v * wide(gain[i:i + ROWS, :].astype(F32), t)

    def token_sum(v):
        return jnp.sum(lane_fold(v), axis=1, keepdims=True).astype(BF16).astype(F32)

    at = lax.broadcasted_iota(jnp.int32, (ROWS, LANES), 1)
    s1 = jnp.zeros((8, t), F32)
    s2 = jnp.zeros((8, t), F32)
    for i in range(0, d, ROWS):
        c, v, g = terms(i)
        s1 += rows_sum(g)
        s2 += rows_sum(g * c)
        acc[i:i + ROWS, :] += jnp.where(at == lane, token_sum(v * c), jnp.where(at == lane + 1, token_sum(v), 0.0))
    m1 = jnp.sum(s1, axis=0, keepdims=True) * (1.0 / d)
    m2 = jnp.sum(s2, axis=0, keepdims=True) * (1.0 / d)
    for i in range(0, d, ROWS):
        c, _, g = terms(i)
        z = (g - m1 - c * m2) * rstd + skip[i:i + ROWS, :].astype(F32)
        dst[i:i + ROWS, :] = z.astype(BF16)


def skewed(jobs, first, second):
    pending = []
    for job in jobs:
        pending.append((job, first(*job)))
        if len(pending) > SKEW:
            job, v = pending.pop(0)
            second(*job, v)
    for job, v in pending:
        second(*job, v)


def f_heads(t, o, p, heads, seq):
    d, n = o.shape
    head = d // heads
    two = 2 * head
    pairs = heads // 2
    key = lax.broadcasted_iota(jnp.int32, (seq, 2 * seq), 0)
    qry = lax.rem(lax.broadcasted_iota(jnp.int32, (seq, 2 * seq), 1), seq)
    ok = key <= qry
    c = (head ** -0.5) * 1.4426950408889634

    def score(b, j):
        r0, lanes = two * j, slice(b * seq, (b + 1) * seq)
        q = t[r0:r0 + two, lanes]
        return dot(t[d + r0:d + r0 + two, lanes], block_diag(q[:head], q[head:]), 0, 0)

    def mix(b, j, s):
        r0, lanes = two * j, slice(b * seq, (b + 1) * seq)
        s = jnp.where(ok, s, -1e30)
        m = jnp.max(s, axis=0, keepdims=True)
        e = jnp.exp2((s - m) * c)
        e = e * (1.0 / jnp.sum(e, axis=0, keepdims=True))
        k0 = (b * pairs + j) * seq
        p[k0:k0 + seq, :] = e
        x = dot(t[2 * d + r0:2 * d + r0 + two, lanes], e.astype(BF16))
        o[r0:r0 + head, lanes] = x[:head, :seq].astype(BF16)
        o[r0 + head:r0 + two, lanes] = x[head:, seq:].astype(BF16)

    skewed([(b, j) for b in range(n // seq) for j in range(pairs)], score, mix)


def b_heads(t, do, dt, p, heads, seq):
    d, n = do.shape
    head = d // heads
    two = 2 * head
    pairs = heads // 2
    scale = head ** -0.5

    def first(b, j):
        r0, lanes = two * j, slice(b * seq, (b + 1) * seq)
        z = do[r0:r0 + two, lanes]
        return dot(t[2 * d + r0:2 * d + r0 + two, lanes], block_diag(z[:head], z[head:]), 0, 0)

    def diag(r0, lanes, x, k):
        dt[r0:r0 + head, lanes] = (x[:head, :seq] * k).astype(BF16)
        dt[r0 + head:r0 + two, lanes] = (x[head:, seq:] * k).astype(BF16)

    def second(b, j, dp):
        r0, lanes = two * j, slice(b * seq, (b + 1) * seq)
        k0 = (b * pairs + j) * seq
        e = p[k0:k0 + seq, :]
        w = e * dp
        ds = (w - e * jnp.sum(w, axis=0, keepdims=True)).astype(BF16)
        eb = e.astype(BF16)
        diag(r0, lanes, dot(t[d + r0:d + r0 + two, lanes], ds), scale)
        tall = jnp.concatenate([ds[:, :seq], ds[:, seq:]], 0)
        diag(d + r0, lanes, dot(t[r0:r0 + two, lanes], tall, 1, 1), scale)
        tall = jnp.concatenate([eb[:, :seq], eb[:, seq:]], 0)
        diag(2 * d + r0, lanes, dot(do[r0:r0 + two, lanes], tall, 1, 1), 1.0)

    skewed([(b, j) for b in range(n // seq) for j in range(pairs)], first, second)


def gelu_and_slope(x):
    x2 = x * x
    hp = 0.5 * jnp.tanh(x * (x2 * K1 + K0)) + 0.5
    u = x * hp
    return u, hp + (u - u * hp) * (x2 * (6.0 * K1) + 2.0 * K0)


class Group:
    def __init__(self, n):
        self.n, self.half, self.last = n, n // 2, n - 1
        self.me = lax.axis_index('pp')
        self.side = self.me // self.half
        self.depth = self.me + self.side * (self.last - 2 * self.me)
        self.inner = self.me + 1 - 2 * self.side
        self.outer = self.me - 1 + 2 * self.side
        self.lead = self.half + 1 - self.depth - self.depth // 2

    def place(self, i):
        far = lax.rem(i - self.half + self.half // 2, self.half) + self.half
        return jnp.where(i < self.half, i, far)

    def step(self, s):
        q = s - self.lead
        pair = q // 2
        even = (q - 2 * pair) == 0
        rest = self.n - self.lead
        head = s < self.lead
        alt = q < 2 * rest
        second = jnp.logical_and(jnp.logical_not(head), jnp.logical_or(jnp.logical_not(alt), even))
        m = jnp.where(head, s, jnp.where(alt, jnp.where(even, pair, self.lead + pair), q - rest))
        return second.astype(jnp.int32), m


def run_phase(g, c_first, src, final, slots, out, load_sems, recv_sems, send_sems, final_sem, feed_sems, weights, unit,
              begin=None):
    n, half = g.n, g.half
    inside = g.depth == half - 1
    outside = g.depth == 0

    def copies_of(c):
        return [pltpu.make_async_copy(h.at[c], v.at[c], load_sems.at[c, i]) for i, (h, v) in enumerate(weights)]

    for c in (c_first, 1 - c_first):
        for w in copies_of(c):
            w.start()
    barrier = pltpu.get_barrier_semaphore()
    for i in range(n):
        pl.semaphore_signal(barrier, inc=1, device_id={'pp': jnp.int32(i)})
    pl.semaphore_wait(barrier, n)
    if begin is not None:
        begin()

    def remote(a, b, send, recv, dev):
        return pltpu.make_async_remote_copy(src_ref=a, dst_ref=b, send_sem=send, recv_sem=recv, device_id={'pp': dev})

    for k, head in ((0, 0), (1, g.last)):
        spot = g.place(g.me + k * (g.last - 2 * g.me))

        @pl.when(g.me == head)
        def _():
            pltpu.make_async_copy(src, slots.at[0, spot], recv_sems.at[0, spot]).start()

        @pl.when(g.me != head)
        def _():
            remote(src, slots.at[0, spot], feed_sems.at[k], recv_sems.at[0, spot], jnp.int32(head)).start()

    def sent(s):
        sec, m = g.step(s)
        kept = jnp.logical_or(jnp.logical_and(sec == 0, inside),
                              jnp.logical_and(jnp.logical_and(sec == 1, outside), m >= half))
        return jnp.logical_not(kept)

    def settle(s):
        @pl.when(sent(s))
        def _():
            par = lax.rem(s, 2)
            remote(out.at[par], slots.at[0, 0], send_sems.at[par], recv_sems.at[0, 0], g.me).wait_send()

    def body(s, carry):
        sec, m = g.step(s)
        c = jnp.where(sec == 1, 1 - c_first, c_first)
        par = lax.rem(s, 2)

        @pl.when(jnp.logical_or(s == 0, s == g.lead))
        def _():
            for w in copies_of(c):
                w.wait()

        @pl.when(s >= 2)
        def _():
            settle(s - 2)

        @pl.when(jnp.logical_not(jnp.logical_and(sec == 1, inside)))
        def _():
            remote(out.at[par], slots.at[sec, m], send_sems.at[par], recv_sems.at[sec, m], g.me).wait_recv()

        unit(s, c, m, slots.at[sec, m], out.at[par])

        @pl.when(jnp.logical_and(sec == 0, inside))
        def _():
            slots[1, m] = out[par]

        @pl.when(jnp.logical_and(sec == 0, jnp.logical_not(inside)))
        def _():
            remote(out.at[par], slots.at[0, m], send_sems.at[par], recv_sems.at[0, m], g.inner).start()

        @pl.when(jnp.logical_and(sec == 1, jnp.logical_not(outside)))
        def _():
            remote(out.at[par], slots.at[1, m], send_sems.at[par], recv_sems.at[1, m], g.outer).start()

        owner = m + g.side * (g.last - 2 * m)
        done = jnp.logical_and(jnp.logical_and(sec == 1, outside), m < half)

        @pl.when(jnp.logical_and(done, owner == g.me))
        def _():
            pltpu.make_async_copy(out.at[par], final, send_sems.at[par]).start()

        @pl.when(jnp.logical_and(done, owner != g.me))
        def _():
            remote(out.at[par], final, send_sems.at[par], final_sem.at[0], owner).start()

        return carry

    lax.fori_loop(0, 2 * n, body, 0)
    settle(2 * n - 2)
    settle(2 * n - 1)
    for k, head in ((0, 0), (1, g.last)):
        @pl.when(g.me != head)
        def _():
            remote(src, slots.at[0, 0], feed_sems.at[k], recv_sems.at[0, 0], jnp.int32(head)).wait_send()

    @pl.when(jnp.logical_not(outside))
    def _():
        remote(out.at[0], final, send_sems.at[0], final_sem.at[0], g.me).wait_recv()


def forward_kernel(n, heads, seq, src, wq, wo, w1, w2, bq, b1, vec,
                   final, hs, ts, rs, ps, gs, ss, as_, os_, bs, us,
                   vwq, vwo, vw1, vw2, vbq, vb1, vvec, slots, out, a, t, o, r, u, pg, stats,
                   load_sems, recv_sems, send_sems, final_sem, feed_sems, sems):
    g = Group(n)
    d, tok = a.shape
    f = u.shape[0]
    prow = ps.shape[2]

    def unit(s, c, m, x, y):
        def save(i, v, dst):
            cp = pltpu.make_async_copy(v, dst.at[c, m], sems.at[i])
            cp.start()
            return cp

        waits = [save(0, x, hs)]
        f_norm(x, vvec.at[c, 0], vvec.at[c, 1], a, stats, 0)
        cp_a = save(1, a, as_)
        v = a[...]
        for i in range(0, 3 * d, CH):
            t[i:i + CH, :] = (dot(vwq[c, i:i + CH, :], v) + wide(vbq[c, i:i + CH, :].astype(F32), tok)).astype(BF16)
        waits.append(save(2, t, ts))
        f_heads(t, o, pg, heads, seq)
        waits.append(save(3, o, os_))
        cp_p = save(4, pg.at[pl.ds(0, prow), :], ps)
        v = o[...]
        for i in range(0, d, CH):
            z = dot(vwo[c, :, i:i + CH], v, 0, 0) + wide(vvec[c, 2, i:i + CH, :].astype(F32), tok)
            r[i:i + CH, :] = (z + x[i:i + CH, :].astype(F32)).astype(BF16)
        waits.append(save(5, r, rs))
        cp_a.wait()
        f_norm(r, vvec.at[c, 3], vvec.at[c, 4], a, stats, 2)
        waits.append(save(6, a, bs))
        waits.append(save(7, stats, ss))
        cp_p.wait()
        v = a[...]
        for i in range(0, f, CH):
            h = dot(vw1[c, :, i:i + CH], v, 0, 0) + wide(vb1[c, i:i + CH, :].astype(F32), tok)
            uu, slope = gelu_and_slope(h)
            u[i:i + CH, :] = uu.astype(BF16)
            pg[i:i + CH, :] = slope[:, :tok // 2]
            pg[f + i:f + i + CH, :] = slope[:, tok // 2:]
        waits.append(save(8, u, us))
        waits.append(save(9, pg, gs))
        v = u[...]
        for i in range(0, d, CH):
            z = dot(vw2[c, :, i:i + CH], v, 0, 0) + wide(vvec[c, 5, i:i + CH, :].astype(F32), tok)
            y[i:i + CH, :] = (z + r[i:i + CH, :].astype(F32)).astype(BF16)
        for w in waits:
            w.wait()

    weights = [(wq, vwq), (wo, vwo), (w1, vw1), (w2, vw2), (bq, vbq), (b1, vb1), (vec, vvec)]
    run_phase(g, g.side, src, final, slots, out, load_sems, recv_sems, send_sems, final_sem, feed_sems, weights, unit)


def backward_kernel(n, heads, seq, src, wq, wo, w1, w2, vec, hs, ts, rs, ps, gs, ss,
                    final, dys, dgs, drs, dts, sums,
                    vwq, vwo, vw1, vw2, vvec, slots, out, h, t, r, dg, dr, dt, pg, stats, acc,
                    load_sems, recv_sems, send_sems, final_sem, feed_sems, in_sems, sems):
    g = Group(n)
    d, tok = h.shape
    f = dg.shape[0]
    prow = ps.shape[2]
    c_first = 1 - g.side

    def fetch(i, s):
        sec, m = g.step(s)
        c = jnp.where(sec == 1, 1 - c_first, c_first)
        hbm, v = ((gs, pg), (ps, pg.at[pl.ds(0, prow), :]), (ts, t), (rs, r), (hs, h), (ss, stats))[i]
        return pltpu.make_async_copy(hbm.at[c, m], v, in_sems.at[i])

    def ahead(i, s):
        @pl.when(s + 1 < 2 * n)
        def _():
            fetch(i, s + 1).start()

    for i in (0, 2, 3, 4, 5):
        fetch(i, 0).start()
    acc[...] = jnp.zeros_like(acc)

    def unit(s, c, m, dy, y):
        def save(i, v, dst):
            cp = pltpu.make_async_copy(v, dst.at[c, m], sems.at[i])
            cp.start()
            return cp

        waits = [save(0, dy, dys)]
        fetch(0, s).wait()
        v = dy[...]
        for i in range(0, f, CH):
            du = dot(vw2[c, i:i + CH, :], v).astype(BF16).astype(F32)
            dg[i:i + CH, :tok // 2] = (du[:, :tok // 2] * pg[i:i + CH, :]).astype(BF16)
            dg[i:i + CH, tok // 2:] = (du[:, tok // 2:] * pg[f + i:f + i + CH, :]).astype(BF16)
        fetch(1, s).start()
        waits.append(save(1, dg, dgs))
        v = dg[...]
        for i in range(0, d, CH):
            y[i:i + CH, :] = dot(vw1[c, i:i + CH, :], v).astype(BF16)
        fetch(3, s).wait()
        fetch(5, s).wait()
        b_norm(y, r, vvec.at[c, 3], dy, dr, stats, 2, acc.at[c], 2)
        ahead(3, s)
        waits.append(save(2, dr, drs))
        v = dr[...]
        for i in range(0, d, CH):
            y[i:i + CH, :] = dot(vwo[c, i:i + CH, :], v).astype(BF16)
        fetch(1, s).wait()
        fetch(2, s).wait()
        b_heads(t, y, dt, pg, heads, seq)
        ahead(0, s)
        ahead(2, s)
        waits.append(save(3, dt, dts))
        v = dt[...]
        for i in range(0, d, CH):
            y[i:i + CH, :] = dot(vwq[c, :, i:i + CH], v, 0, 0).astype(BF16)
        fetch(4, s).wait()
        b_norm(y, h, vvec.at[c, 0], dr, y, stats, 0, acc.at[c], 0)
        ahead(4, s)
        ahead(5, s)
        for w in waits:
            w.wait()

    weights = [(wq, vwq), (wo, vwo), (w1, vw1), (w2, vw2), (vec, vvec)]
    run_phase(g, c_first, src, final, slots, out, load_sems, recv_sems, send_sems, final_sem, feed_sems, weights, unit)
    cp = pltpu.make_async_copy(acc, sums, sems.at[0])
    cp.start()
    cp.wait()


def run_forward(mesh, heads, seq, xt, weights):
    n = mesh.shape['pp']
    wq, wo, w1, w2, bq, b1, vec = weights
    d, tok = xt.shape
    f = w1.shape[2]
    prow = (tok // seq) * (heads // 2) * seq
    st = jax.ShapeDtypeStruct
    outs = [st((d, tok), BF16)] + [st((2, n) + v, k) for v, k in (
        ((d, tok), BF16), ((3 * d, tok), BF16), ((d, tok), BF16), ((prow, 2 * seq), F32), ((2 * f, tok // 2), F32),
        ((8, tok), F32), ((d, tok), BF16), ((d, tok), BF16), ((d, tok), BF16), ((f, tok), BF16))]
    vm = pltpu.VMEM
    scratch = [vm(w.shape, w.dtype) for w in weights] + [
        vm((2, n, d, tok), BF16), vm((2, d, tok), BF16), vm((d, tok), BF16), vm((3 * d, tok), BF16),
        vm((d, tok), BF16), vm((d, tok), BF16), vm((f, tok), BF16), vm((2 * f, tok // 2), F32), vm((8, tok), F32),
        pltpu.SemaphoreType.DMA((2, 7)), pltpu.SemaphoreType.DMA((2, n)), pltpu.SemaphoreType.DMA((2,)),
        pltpu.SemaphoreType.DMA((1,)), pltpu.SemaphoreType.DMA((2,)), pltpu.SemaphoreType.DMA((10,))]
    return pl.pallas_call(
        functools.partial(forward_kernel, n, heads, seq), out_shape=outs, in_specs=[HBM] * 8, out_specs=[HBM] * 11,
        scratch_shapes=scratch, name='forward_walk',
        compiler_params=pltpu.CompilerParams(vmem_limit_bytes=VMEM_LIMIT, collective_id=0, has_side_effects=True),
    )(xt, *weights)


def run_backward(mesh, heads, seq, dyt, weights, stash):
    n = mesh.shape['pp']
    wq, wo, w1, w2, _, _, vec = weights
    d, tok = dyt.shape
    f = w1.shape[2]
    st = jax.ShapeDtypeStruct
    outs = [st((d, tok), BF16)] + [st((2, n) + v, BF16) for v in ((d, tok), (f, tok), (d, tok), (3 * d, tok))]
    outs += [st((2, d, LANES), F32)]
    vm = pltpu.VMEM
    ws = (wq, wo, w1, w2, vec)
    scratch = [vm(w.shape, w.dtype) for w in ws] + [
        vm((2, n, d, tok), BF16), vm((2, d, tok), BF16), vm((d, tok), BF16), vm((3 * d, tok), BF16),
        vm((d, tok), BF16), vm((f, tok), BF16), vm((d, tok), BF16), vm((3 * d, tok), BF16),
        vm((2 * f, tok // 2), F32), vm((8, tok), F32), vm((2, d, LANES), F32),
        pltpu.SemaphoreType.DMA((2, 5)), pltpu.SemaphoreType.DMA((2, n)), pltpu.SemaphoreType.DMA((2,)),
        pltpu.SemaphoreType.DMA((1,)), pltpu.SemaphoreType.DMA((2,)), pltpu.SemaphoreType.DMA((6,)),
        pltpu.SemaphoreType.DMA((4,))]
    return pl.pallas_call(
        functools.partial(backward_kernel, n, heads, seq), out_shape=outs, in_specs=[HBM] * 12, out_specs=[HBM] * 6,
        scratch_shapes=scratch, name='backward_walk',
        compiler_params=pltpu.CompilerParams(vmem_limit_bytes=VMEM_LIMIT, collective_id=1, has_side_effects=True),
    )(dyt, *ws, *stash)


def weight_kernel(token_rows, lhs, rhs, out, side):
    m = pl.program_id(1)
    rows = out.shape[1]
    two = lhs.shape[1]

    def rounded(k, x):
        return dot(x, rhs[0, k], 1, 1).astype(BF16).astype(F32)

    def go(fresh):
        for i in range(0, rows, CH):
            z = 0.0 if fresh else out[0, i:i + CH, :]
            if i == 0 and token_rows:
                e = 0.0 if fresh else side[0]
                for k in range(two):
                    x = jnp.concatenate([lhs[0, k, i:i + CH, :], jnp.ones((16, lhs.shape[3]), BF16)], 0)
                    v = rounded(k, x)
                    z = z + v[:CH]
                    e = e + v[CH:CH + 8]
                side[0] = e
            else:
                for k in range(two):
                    z = z + rounded(k, lhs[0, k, i:i + CH, :])
            out[0, i:i + CH, :] = z
            if not token_rows:
                e = 0.0 if fresh else side[0, i:i + CH, :]
                for k in range(two):
                    v = lane_fold(lhs[0, k, i:i + CH, :].astype(F32))
                    e = e + jnp.sum(v, axis=1, keepdims=True).astype(BF16).astype(F32)
                side[0, i:i + CH, :] = jnp.broadcast_to(e, (CH, LANES))

    @pl.when(m == 0)
    def _():
        go(True)

    @pl.when(m > 0)
    def _():
        go(False)


def weight_grad(lhs, rhs, token_rows, name):
    c, n, rows, tok = lhs.shape
    cols = rhs.shape[2]
    two = 2
    side = (8, cols) if token_rows else (rows, LANES)
    return pl.pallas_call(
        functools.partial(weight_kernel, token_rows), grid=(c, n // two),
        out_shape=[jax.ShapeDtypeStruct((c, rows, cols), F32), jax.ShapeDtypeStruct((c,) + side, F32)],
        in_specs=[pl.BlockSpec((1, two, rows, tok), lambda i, j: (i, j, 0, 0)),
                  pl.BlockSpec((1, two, cols, tok), lambda i, j: (i, j, 0, 0))],
        out_specs=[pl.BlockSpec((1, rows, cols), lambda i, j: (i, 0, 0)),
                   pl.BlockSpec((1,) + side, lambda i, j: (i, 0, 0))],
        name=name,
        compiler_params=pltpu.CompilerParams(vmem_limit_bytes=VMEM_LIMIT, dimension_semantics=('arbitrary', 'arbitrary')),
    )(lhs, rhs)


def solution(mesh):
    data_spec = P(('dp', 'pp'))
    weight_spec = P('pp')

    def per_device(x, dy, w_qkv, w_attn, w_fc, w_proj, b_qkv, b_fc, vec_d):
        _, batch, seq, d = x.shape
        heads = w_qkv.shape[5]
        tok = batch * seq

        def column(v):
            return jnp.broadcast_to(v[..., None], v.shape + (LANES,))

        weights = (
            w_qkv.reshape(2, d, 3 * d).transpose(0, 2, 1), w_attn.reshape(2, d, d), w_fc[0, :, 0], w_proj[0, :, 0],
            column(b_qkv.reshape(2, 3 * d)), column(b_fc.reshape(2, -1)), column(vec_d[0, :, 0]))
        xt = x.reshape(tok, d).T
        dyt = dy.reshape(tok, d).T
        yt, hs, ts, rs, ps, gs, ss, as_, os_, bs, us = run_forward(mesh, heads, seq, xt, weights)
        dxt, dys, dgs, drs, dts, sums = run_backward(mesh, heads, seq, dyt, weights, (hs, ts, rs, ps, gs, ss))
        gq, gbq = weight_grad(dts, as_, False, 'grad_qkv')
        go, gbo = weight_grad(os_, drs, True, 'grad_attn')
        g1, gb1 = weight_grad(bs, dgs, True, 'grad_fc')
        g2, gb2 = weight_grad(us, dys, True, 'grad_proj')
        s = sums[:, :, :4].transpose(0, 2, 1)
        gv = jnp.stack([s[:, 0], s[:, 1], gbo[:, 0], s[:, 2], s[:, 3], gb2[:, 0]], axis=1)
        back = lambda v: v.T.reshape(x.shape)
        return (back(yt), back(dxt),
                gq.transpose(0, 2, 1).reshape(w_qkv.shape), go.reshape(w_attn.shape), g1.reshape(w_fc.shape),
                g2.reshape(w_proj.shape), gbq[:, :, 0].reshape(b_qkv.shape), gb1[:, 0].reshape(b_fc.shape),
                gv.reshape(vec_d.shape))

    return jax.shard_map(per_device, mesh=mesh, in_specs=(data_spec, data_spec) + (weight_spec,) * 7,
                         out_specs=(data_spec, data_spec) + (data_spec,) * 7, check_vma=False)
```

time: 4220 us -> 955 us (0.23)
  waiting for transfers between devices: 1600 us -> 0 us
  starting transfers between devices: 918 us -> 0 us
  Pallas kernels: 0 us -> 917 us
  matrix products: 594 us -> 0 us
  local copies, waits for them, and re-layouts: 586 us -> 26.4 us
  other arithmetic: 402 us -> 0.03 us
  loops' own time: 86 us -> 0 us
    ppermute x58 -> x0, waiting for transfers between devices: 1590 us -> none  [the longest x7 584 us: per_device(): peer_down = tuple((lax.ppermute(g, 'pp', opposite) for g in down_acc))]
    ppermute x58 -> x0, starting transfers between devices: 917 us -> none  [the longest x11 605 us: backward_step(): down_cot_in = lax.ppermute(down_dx, 'pp', to_prev)]
    pallas_call x0 -> x6, Pallas kernels: none -> 917 us  [the longest x1 406 us: run_forward(): pl.pallas_call(functools.partial(forward_kernel, n, heads, seq), out_shap...]
    dot_general x184 -> x0, matrix products: 594 us -> none  [the longest x24 217 us: gpt_layer(): jnp.dot(hidden, w_proj, preferred_element_type=jnp.float32)]
    convert_element_type x112 -> x0, local copies, waits for them, and re-layouts: 157 us -> none  [the longest x8 64.8 us: stage_backward(): g.astype(jnp.float32)]
    add x40 -> x0, other arithmetic: 113 us -> none  [stage_backward(): a + g.astype(jnp.float32)]
    dynamic_update_slice x44 -> x0, local copies, waits for them, and re-layouts: 91.1 us -> none  [store_row(): return lax.dynamic_update_index_in_dim(buffer, row_val, index, 0)]
    reduce_sum x96 -> x0, other arithmetic: 86.4 us -> none  [the longest x24 32.4 us: layer_norm(): scaled * ln_gain.astype(jnp.float32) + ln_shift.astype(jnp.float32)]
  transfers between devices with their start and end apart: 62 -> 0, of which waited for: 16 -> 0; matrix products, arithmetic and copies ran while one was open for 37% -> 0% of each run, Pallas kernels for 0% -> 0%
where the time goes in v1:
time: 955 us; the launch traced here: 945 us
  Pallas kernels  917 us (96%)
  local copies, waits for them, and re-layouts  26.4 us (3%)
    pallas_call x1, Pallas kernels, run_forward(): pl.pallas_call(functools.partial(forward_kernel, n, heads, seq), out_shap...  406 us
    pallas_call x1, Pallas kernels, run_backward(): pl.pallas_call(functools.partial(backward_kernel, n, heads, seq), out_sha...  352 us
    pallas_call x4, Pallas kernels, weight_grad(): pl.pallas_call(functools.partial(weight_kernel, token_rows), grid=(c, n /...  160 us

profile of v1, /device:TPU:127, one launch (start us, length us, event | category | flops | bytes accessed | tf_op | source)
XLA Modules:
  0.0 944.5 jit_solution(1574645266480902834)
XLA Ops:
  0.6 0.8 broadcast_in_dim.21
  1.5 0.7 copy.45
  2.2 2.3 copy.59
  4.5 2.3 copy.61
  6.8 1.6 broadcast_in_dim.22.bq
  8.4 2.5 broadcast_in_dim.24.b1
  10.9 2.7 broadcast_in_dim.26.vec
  13.6 405.6 %forward_walk.1 = (bf16[768,512]{1,0:T(8,128)(2,1)}, bf16[2,8,768,512]{3,2,1,0:T(8,128)(2,1)}, bf16[2,8,2304,512]{3,2,1,0:T(8,128)(2,1)}, bf16[2,8,768,512]{3,2,...) custom-call(bf16[768,512]{1,0:T(8,128)(2,1)} %bitcast.48, ...), custom_call_target="tpu_custom_call" | custom-call | tf_op jit(solution)/shard_map/forward_walk/pallas_call | solution.py:448
  419.3 2.3 copy.60
  421.5 351.6 %backward_walk.1 = (bf16[768,512]{1,0:T(8,128)(2,1)}, bf16[2,8,768,512]{3,2,1,0:T(8,128)(2,1)}, bf16[2,8,3072,512]{3,2,1,0:T(8,128)(2,1)}, bf16[2,8,768,512]{3,2...) custom-call(bf16[768,512]{1,0:T(8,128)(2,1)} %bitcast.47, bf16[2,2304,768]{2,1,0:T(8,128)(2,1)} %bitcast.44, ...), custom_call_target="tpu_custom_call" | custom-call | tf_op jit(solution)/shard_map/backward_walk/pallas_call | solution.py:472
  773.2 50.0 %grad_proj.1 = (f32[2,3072,768]{2,1,0:T(8,128)}, f32[2,8,768]{2,1,0:T(8,128)}) custom-call(bf16[2,8,3072,512]{3,2,1,0:T(8,128)(2,1)} %get-tuple-element.51.lhs, bf16[2,8,768,512]{3,2,1,0:T(8,128)(2,1)} %get-tuple-element.52.rhs), custom_call_target="tpu_custom_call" | custom-call | tf_op jit(solution)/shard_map/grad_proj/pallas_call | solution.py:523
  823.2 17.6 %grad_attn.1 = (f32[2,768,768]{2,1,0:T(8,128)}, f32[2,8,768]{2,1,0:T(8,128)}) custom-call(bf16[2,8,768,512]{3,2,1,0:T(8,128)(2,1)} %get-tuple-element.45.lhs, bf16[2,8,768,512]{3,2,1,0:T(8,128)(2,1)} %get-tuple-element.46.rhs), custom_call_target="tpu_custom_call" | custom-call | tf_op jit(solution)/shard_map/grad_attn/pallas_call | solution.py:523
  840.8 2.3 copy.62
  843.1 0.8 slice.29
  843.9 0.8 slice.31
  844.7 1.2 slice_bitcast_fusion
  845.9 0.3 fusion
  846.4 0.3 copy.49
  846.7 0.7 copy.58
  847.4 41.2 %grad_qkv.1 = (f32[2,2304,768]{2,1,0:T(8,128)}, f32[2,2304,128]{2,1,0:T(8,128)}) custom-call(bf16[2,8,2304,512]{3,2,1,0:T(8,128)(2,1)} %get-tuple-element.42.lhs, bf16[2,8,768,512]{3,2,1,0:T(8,128)(2,1)} %get-tuple-element.43.rhs), custom_call_target="tpu_custom_call" | custom-call | tf_op jit(solution)/shard_map/grad_qkv/pallas_call | solution.py:523
  888.6 2.4 slice_reduce_fusion
  891.0 0.7 reshape_squeeze.6
  891.7 50.8 %grad_fc.1 = (f32[2,768,3072]{2,1,0:T(8,128)}, f32[2,8,3072]{2,1,0:T(8,128)}) custom-call(bf16[2,8,768,512]{3,2,1,0:T(8,128)(2,1)} %get-tuple-element.48.lhs, bf16[2,8,3072,512]{3,2,1,0:T(8,128)(2,1)} %get-tuple-element.49.rhs), custom_call_target="tpu_custom_call" | custom-call | tf_op jit(solution)/shard_map/grad_fc/pallas_call | solution.py:523
  942.5 1.5 slice_bitcast_fusion.1
  (4 shorter events, 0.3 us)

commit v2 on v1

--- a/solution.py
+++ b/solution.py
@@ -13,7 +13,7 @@
 LANES = 128
 ROWS = 96
 CH = 256
-SKEW = 3
+SKEW = 8
 K0 = 0.7978845608028654
 K1 = K0 * 0.044715
 VMEM_LIMIT = 67043328
@@ -29,12 +29,16 @@
     return jnp.sum(v.reshape(r // 8, 8, t), axis=0)
 
 
-def wide(col, t):
-    return jnp.concatenate([col] * (t // LANES), axis=1)
+def column(cols, lane, row, count):
+    return cols[row:row + count, lane:lane + 1].astype(F32)
 
 
 def lane_fold(v):
     return functools.reduce(jnp.add, [v[:, k:k + LANES] for k in range(0, v.shape[1], LANES)])
+
+
+def token_sum(v):
+    return jnp.sum(lane_fold(v), axis=1, keepdims=True).astype(BF16).astype(F32)
 
 
 def block_diag(a, b):
@@ -42,7 +46,7 @@
     return jnp.concatenate([jnp.concatenate([a, z], 1), jnp.concatenate([z, b], 1)], 0)
 
 
-def f_norm(src, gain, shift, dst, stats, row):
+def f_norm(src, cols, lane, dst, stats, row):
     d, t = src.shape
     acc = jnp.zeros((8, t), F32)
     for i in range(0, d, ROWS):
@@ -55,14 +59,12 @@
     rstd = lax.rsqrt(jnp.sum(acc, axis=0, keepdims=True) * (1.0 / d) + EPS)
     for i in range(0, d, ROWS):
         c = (src[i:i + ROWS, :].astype(F32) - mean) * rstd
-        g = wide(gain[i:i + ROWS, :].astype(F32), t)
-        s = wide(shift[i:i + ROWS, :].astype(F32), t)
-        dst[i:i + ROWS, :] = (c * g + s).astype(BF16)
+        dst[i:i + ROWS, :] = (c * column(cols, lane, i, ROWS) + column(cols, lane + 1, i, ROWS)).astype(BF16)
     stats[row:row + 1, :] = mean
     stats[row + 1:row + 2, :] = rstd
 
 
-def b_norm(dn, src, gain, skip, dst, stats, row, acc, lane):
+def b_norm(dn, src, cols, gain, skip, dst, stats, row, acc, lane):
     d, t = src.shape
     mean = stats[row:row + 1, :]
     rstd = stats[row + 1:row + 2, :]
@@ -70,10 +72,7 @@
     def terms(i):
         c = (src[i:i + ROWS, :].astype(F32) - mean) * rstd
         v = dn[i:i + ROWS, :].astype(F32)
-        return c, v, v * wide(gain[i:i + ROWS, :].astype(F32), t)
-
-    def token_sum(v):
-        return jnp.sum(lane_fold(v), axis=1, keepdims=True).astype(BF16).astype(F32)
+        return c, v, v * column(cols, gain, i, ROWS)
 
     at = lax.broadcasted_iota(jnp.int32, (ROWS, LANES), 1)
     s1 = jnp.zeros((8, t), F32)
@@ -102,7 +101,7 @@
         second(*job, v)
 
 
-def f_heads(t, o, p, heads, seq):
+def f_heads(t, o, p, heads, seq, after):
     d, n = o.shape
     head = d // heads
     two = 2 * head
@@ -128,11 +127,13 @@
         x = dot(t[2 * d + r0:2 * d + r0 + two, lanes], e.astype(BF16))
         o[r0:r0 + head, lanes] = x[:head, :seq].astype(BF16)
         o[r0 + head:r0 + two, lanes] = x[head:, seq:].astype(BF16)
+        if j == pairs - 1:
+            after(b)
 
     skewed([(b, j) for b in range(n // seq) for j in range(pairs)], score, mix)
 
 
-def b_heads(t, do, dt, p, heads, seq):
+def b_heads(t, do, dt, p, heads, seq, after):
     d, n = do.shape
     head = d // heads
     two = 2 * head
@@ -160,6 +161,8 @@
         diag(d + r0, lanes, dot(t[r0:r0 + two, lanes], tall, 1, 1), scale)
         tall = jnp.concatenate([eb[:, :seq], eb[:, seq:]], 0)
         diag(2 * d + r0, lanes, dot(do[r0:r0 + two, lanes], tall, 1, 1), 1.0)
+        if j == pairs - 1:
+            after(b)
 
     skewed([(b, j) for b in range(n // seq) for j in range(pairs)], first, second)
 
@@ -300,129 +303,160 @@
         remote(out.at[0], final, send_sems.at[0], final_sem.at[0], g.me).wait_recv()
 
 
-def forward_kernel(n, heads, seq, src, wq, wo, w1, w2, bq, b1, vec,
+def forward_kernel(n, heads, seq, src, wq, wo, w1, w2, cols,
                    final, hs, ts, rs, ps, gs, ss, as_, os_, bs, us,
-                   vwq, vwo, vw1, vw2, vbq, vb1, vvec, slots, out, a, t, o, r, u, pg, stats,
+                   vwq, vwo, vw1, vw2, vcols, slots, out, a, t, o, r, u, pg, ya, stats,
                    load_sems, recv_sems, send_sems, final_sem, feed_sems, sems):
     g = Group(n)
     d, tok = a.shape
     f = u.shape[0]
-    prow = ps.shape[2]
+    half = tok // 2
+    part = ps.shape[2] // (tok // seq)
 
     def unit(s, c, m, x, y):
-        def save(i, v, dst):
-            cp = pltpu.make_async_copy(v, dst.at[c, m], sems.at[i])
-            cp.start()
-            return cp
-
-        waits = [save(0, x, hs)]
-        f_norm(x, vvec.at[c, 0], vvec.at[c, 1], a, stats, 0)
-        cp_a = save(1, a, as_)
+        def copy(i, v, dst, at=None):
+            hbm = dst.at[c, m]
+            if at is not None:
+                v, hbm = v.at[pl.ds(*at), :], hbm.at[pl.ds(*at), :]
+            return pltpu.make_async_copy(v, hbm, sems.at[i])
+
+        cv = vcols.at[c]
+        copy(0, x, hs).start()
+        f_norm(x, cv, 0, a, stats, 0)
+        copy(1, a, as_).start()
         v = a[...]
         for i in range(0, 3 * d, CH):
-            t[i:i + CH, :] = (dot(vwq[c, i:i + CH, :], v) + wide(vbq[c, i:i + CH, :].astype(F32), tok)).astype(BF16)
-        waits.append(save(2, t, ts))
-        f_heads(t, o, pg, heads, seq)
-        waits.append(save(3, o, os_))
-        cp_p = save(4, pg.at[pl.ds(0, prow), :], ps)
+            z = dot(vwq[c, i:i + CH, :], v) + column(cv, 6 + i // d, i % d, CH)
+            t[i:i + CH, :] = z.astype(BF16)
+        copy(2, t, ts).start()
+        f_heads(t, o, pg, heads, seq, lambda b: copy(4, pg, ps, (b * part, part)).start())
+        copy(3, o, os_).start()
         v = o[...]
         for i in range(0, d, CH):
-            z = dot(vwo[c, :, i:i + CH], v, 0, 0) + wide(vvec[c, 2, i:i + CH, :].astype(F32), tok)
-            r[i:i + CH, :] = (z + x[i:i + CH, :].astype(F32)).astype(BF16)
-        waits.append(save(5, r, rs))
-        cp_a.wait()
-        f_norm(r, vvec.at[c, 3], vvec.at[c, 4], a, stats, 2)
-        waits.append(save(6, a, bs))
-        waits.append(save(7, stats, ss))
-        cp_p.wait()
+            z = dot(vwo[c, :, i:i + CH], v, 0, 0) + column(cv, 2, i, CH) + x[i:i + CH, :].astype(F32)
+            r[i:i + CH, :] = z.astype(BF16)
+        copy(5, r, rs).start()
+        copy(1, a, as_).wait()
+        f_norm(r, cv, 3, a, stats, 2)
+        copy(6, a, bs).start()
+        copy(7, stats, ss).start()
+        copy(4, pg.at[pl.ds(0, ps.shape[2]), :], ps).wait()
         v = a[...]
-        for i in range(0, f, CH):
-            h = dot(vw1[c, :, i:i + CH], v, 0, 0) + wide(vb1[c, i:i + CH, :].astype(F32), tok)
-            uu, slope = gelu_and_slope(h)
-            u[i:i + CH, :] = uu.astype(BF16)
-            pg[i:i + CH, :] = slope[:, :tok // 2]
-            pg[f + i:f + i + CH, :] = slope[:, tok // 2:]
-        waits.append(save(8, u, us))
-        waits.append(save(9, pg, gs))
-        v = u[...]
-        for i in range(0, d, CH):
-            z = dot(vw2[c, :, i:i + CH], v, 0, 0) + wide(vvec[c, 5, i:i + CH, :].astype(F32), tok)
-            y[i:i + CH, :] = (z + r[i:i + CH, :].astype(F32)).astype(BF16)
-        for w in waits:
-            w.wait()
-
-    weights = [(wq, vwq), (wo, vwo), (w1, vw1), (w2, vw2), (bq, vbq), (b1, vb1), (vec, vvec)]
+
+        def up(k):
+            for i in range(k * d, (k + 1) * d, CH):
+                h = dot(vw1[c, :, i:i + CH], v, 0, 0) + column(cv, 9 + k, i % d, CH)
+                uu, slope = gelu_and_slope(h)
+                u[i:i + CH, :] = uu.astype(BF16)
+                pg[2 * i:2 * i + CH, :] = slope[:, :half]
+                pg[2 * i + CH:2 * i + 2 * CH, :] = slope[:, half:]
+                copy(8, u, us, (i, CH)).start()
+                copy(9, pg, gs, (2 * i, 2 * CH)).start()
+
+        def down(k):
+            w = u[k * d:(k + 1) * d, :]
+            for i in range(0, d, CH):
+                z = dot(vw2[c, k * d:(k + 1) * d, i:i + CH], w, 0, 0)
+                z += (column(cv, 5, i, CH) + r[i:i + CH, :].astype(F32)) if k == 0 else ya[i:i + CH, :]
+                if (k + 1) * d < f:
+                    ya[i:i + CH, :] = z
+                else:
+                    y[i:i + CH, :] = z.astype(BF16)
+
+        up(0)
+        for k in range(1, f // d):
+            up(k)
+            down(k - 1)
+        down(f // d - 1)
+        for i, v, dst in ((0, x, hs), (2, t, ts), (3, o, os_), (5, r, rs), (6, a, bs), (7, stats, ss), (8, u, us),
+                          (9, pg, gs)):
+            copy(i, v, dst).wait()
+
+    weights = [(wq, vwq), (wo, vwo), (w1, vw1), (w2, vw2), (cols, vcols)]
     run_phase(g, g.side, src, final, slots, out, load_sems, recv_sems, send_sems, final_sem, feed_sems, weights, unit)
 
 
-def backward_kernel(n, heads, seq, src, wq, wo, w1, w2, vec, hs, ts, rs, ps, gs, ss,
+def backward_kernel(n, heads, seq, src, wq, wo, w1, w2, cols, hs, ts, rs, ps, gs, ss,
                     final, dys, dgs, drs, dts, sums,
-                    vwq, vwo, vw1, vw2, vvec, slots, out, h, t, r, dg, dr, dt, pg, stats, acc,
+                    vwq, vwo, vw1, vw2, vcols, slots, out, h, t, r, dg, dr, dt, pg, stats, acc,
                     load_sems, recv_sems, send_sems, final_sem, feed_sems, in_sems, sems):
     g = Group(n)
     d, tok = h.shape
     f = dg.shape[0]
+    half = tok // 2
     prow = ps.shape[2]
+    part = prow // (tok // seq)
     c_first = 1 - g.side
 
-    def fetch(i, s):
+    def fetch(i, s, at=None):
         sec, m = g.step(s)
         c = jnp.where(sec == 1, 1 - c_first, c_first)
         hbm, v = ((gs, pg), (ps, pg.at[pl.ds(0, prow), :]), (ts, t), (rs, r), (hs, h), (ss, stats))[i]
-        return pltpu.make_async_copy(hbm.at[c, m], v, in_sems.at[i])
-
-    def ahead(i, s):
+        hbm = hbm.at[c, m]
+        if at is not None:
+            hbm, v = hbm.at[pl.ds(*at), :], v.at[pl.ds(*at), :]
+        return pltpu.make_async_copy(hbm, v, in_sems.at[i])
+
+    def ahead(i, s, at=None):
         @pl.when(s + 1 < 2 * n)
         def _():
-            fetch(i, s + 1).start()
+            fetch(i, s + 1, at).start()
 
     for i in (0, 2, 3, 4, 5):
         fetch(i, 0).start()
     acc[...] = jnp.zeros_like(acc)
 
     def unit(s, c, m, dy, y):
-        def save(i, v, dst):
-            cp = pltpu.make_async_copy(v, dst.at[c, m], sems.at[i])
-            cp.start()
-            return cp
-
-        waits = [save(0, dy, dys)]
+        def copy(i, v, dst, at=None):
+            hbm = dst.at[c, m]
+            if at is not None:
+                v, hbm = v.at[pl.ds(*at), :], hbm.at[pl.ds(*at), :]
+            return pltpu.make_async_copy(v, hbm, sems.at[i])
+
+        cv = vcols.at[c]
+        copy(0, dy, dys).start()
         fetch(0, s).wait()
         v = dy[...]
         for i in range(0, f, CH):
             du = dot(vw2[c, i:i + CH, :], v).astype(BF16).astype(F32)
-            dg[i:i + CH, :tok // 2] = (du[:, :tok // 2] * pg[i:i + CH, :]).astype(BF16)
-            dg[i:i + CH, tok // 2:] = (du[:, tok // 2:] * pg[f + i:f + i + CH, :]).astype(BF16)
+            dg[i:i + CH, :half] = (du[:, :half] * pg[2 * i:2 * i + CH, :]).astype(BF16)
+            dg[i:i + CH, half:] = (du[:, half:] * pg[2 * i + CH:2 * i + 2 * CH, :]).astype(BF16)
         fetch(1, s).start()
-        waits.append(save(1, dg, dgs))
+        ahead(0, s, (prow, 2 * f - prow))
+        copy(1, dg, dgs).start()
         v = dg[...]
         for i in range(0, d, CH):
             y[i:i + CH, :] = dot(vw1[c, i:i + CH, :], v).astype(BF16)
         fetch(3, s).wait()
         fetch(5, s).wait()
-        b_norm(y, r, vvec.at[c, 3], dy, dr, stats, 2, acc.at[c], 2)
+        b_norm(y, r, cv, 3, dy, dr, stats, 2, acc.at[c], 2)
         ahead(3, s)
-        waits.append(save(2, dr, drs))
+        copy(2, dr, drs).start()
         v = dr[...]
         for i in range(0, d, CH):
             y[i:i + CH, :] = dot(vwo[c, i:i + CH, :], v).astype(BF16)
         fetch(1, s).wait()
         fetch(2, s).wait()
-        b_heads(t, y, dt, pg, heads, seq)
-        ahead(0, s)
+        b_heads(t, y, dt, pg, heads, seq, lambda b: ahead(0, s, (b * part, part)))
         ahead(2, s)
-        waits.append(save(3, dt, dts))
+        copy(3, dt, dts).start()
         v = dt[...]
+        at = lax.broadcasted_iota(jnp.int32, (ROWS, LANES), 1)
         for i in range(0, d, CH):
             y[i:i + CH, :] = dot(vwq[c, :, i:i + CH], v, 0, 0).astype(BF16)
+        for i in range(0, d, ROWS):
+            e = 0.0
+            for k in range(3):
+                e = jnp.where(at == 4 + k, token_sum(dt[k * d + i:k * d + i + ROWS, :].astype(F32)), e)
+            acc[c, i:i + ROWS, :] += e
         fetch(4, s).wait()
-        b_norm(y, h, vvec.at[c, 0], dr, y, stats, 0, acc.at[c], 0)
+        b_norm(y, h, cv, 0, dr, y, stats, 0, acc.at[c], 0)
         ahead(4, s)
         ahead(5, s)
-        for w in waits:
-            w.wait()
-
-    weights = [(wq, vwq), (wo, vwo), (w1, vw1), (w2, vw2), (vec, vvec)]
+        for i, v, dst in ((0, dy, dys), (1, dg, dgs), (2, dr, drs), (3, dt, dts)):
+            copy(i, v, dst).wait()
+
+    weights = [(wq, vwq), (wo, vwo), (w1, vw1), (w2, vw2), (cols, vcols)]
     run_phase(g, c_first, src, final, slots, out, load_sems, recv_sems, send_sems, final_sem, feed_sems, weights, unit)
     cp = pltpu.make_async_copy(acc, sums, sems.at[0])
     cp.start()
@@ -431,9 +465,8 @@
 
 def run_forward(mesh, heads, seq, xt, weights):
     n = mesh.shape['pp']
-    wq, wo, w1, w2, bq, b1, vec = weights
     d, tok = xt.shape
-    f = w1.shape[2]
+    f = weights[2].shape[2]
     prow = (tok // seq) * (heads // 2) * seq
     st = jax.ShapeDtypeStruct
     outs = [st((d, tok), BF16)] + [st((2, n) + v, k) for v, k in (
@@ -442,11 +475,12 @@
     vm = pltpu.VMEM
     scratch = [vm(w.shape, w.dtype) for w in weights] + [
         vm((2, n, d, tok), BF16), vm((2, d, tok), BF16), vm((d, tok), BF16), vm((3 * d, tok), BF16),
-        vm((d, tok), BF16), vm((d, tok), BF16), vm((f, tok), BF16), vm((2 * f, tok // 2), F32), vm((8, tok), F32),
-        pltpu.SemaphoreType.DMA((2, 7)), pltpu.SemaphoreType.DMA((2, n)), pltpu.SemaphoreType.DMA((2,)),
+        vm((d, tok), BF16), vm((d, tok), BF16), vm((f, tok), BF16), vm((2 * f, tok // 2), F32), vm((d, tok), F32),
+        vm((8, tok), F32),
+        pltpu.SemaphoreType.DMA((2, 5)), pltpu.SemaphoreType.DMA((2, n)), pltpu.SemaphoreType.DMA((2,)),
         pltpu.SemaphoreType.DMA((1,)), pltpu.SemaphoreType.DMA((2,)), pltpu.SemaphoreType.DMA((10,))]
     return pl.pallas_call(
-        functools.partial(forward_kernel, n, heads, seq), out_shape=outs, in_specs=[HBM] * 8, out_specs=[HBM] * 11,
+        functools.partial(forward_kernel, n, heads, seq), out_shape=outs, in_specs=[HBM] * 6, out_specs=[HBM] * 11,
         scratch_shapes=scratch, name='forward_walk',
         compiler_params=pltpu.CompilerParams(vmem_limit_bytes=VMEM_LIMIT, collective_id=0, has_side_effects=True),
     )(xt, *weights)
@@ -454,15 +488,13 @@
 
 def run_backward(mesh, heads, seq, dyt, weights, stash):
     n = mesh.shape['pp']
-    wq, wo, w1, w2, _, _, vec = weights
     d, tok = dyt.shape
-    f = w1.shape[2]
+    f = weights[2].shape[2]
     st = jax.ShapeDtypeStruct
     outs = [st((d, tok), BF16)] + [st((2, n) + v, BF16) for v in ((d, tok), (f, tok), (d, tok), (3 * d, tok))]
     outs += [st((2, d, LANES), F32)]
     vm = pltpu.VMEM
-    ws = (wq, wo, w1, w2, vec)
-    scratch = [vm(w.shape, w.dtype) for w in ws] + [
+    scratch = [vm(w.shape, w.dtype) for w in weights] + [
         vm((2, n, d, tok), BF16), vm((2, d, tok), BF16), vm((d, tok), BF16), vm((3 * d, tok), BF16),
         vm((d, tok), BF16), vm((f, tok), BF16), vm((d, tok), BF16), vm((3 * d, tok), BF16),
         vm((2 * f, tok // 2), F32), vm((8, tok), F32), vm((2, d, LANES), F32),
@@ -473,63 +505,107 @@
         functools.partial(backward_kernel, n, heads, seq), out_shape=outs, in_specs=[HBM] * 12, out_specs=[HBM] * 6,
         scratch_shapes=scratch, name='backward_walk',
         compiler_params=pltpu.CompilerParams(vmem_limit_bytes=VMEM_LIMIT, collective_id=1, has_side_effects=True),
-    )(dyt, *ws, *stash)
-
-
-def weight_kernel(token_rows, lhs, rhs, out, side):
-    m = pl.program_id(1)
-    rows = out.shape[1]
-    two = lhs.shape[1]
-
-    def rounded(k, x):
-        return dot(x, rhs[0, k], 1, 1).astype(BF16).astype(F32)
-
-    def go(fresh):
-        for i in range(0, rows, CH):
-            z = 0.0 if fresh else out[0, i:i + CH, :]
-            if i == 0 and token_rows:
-                e = 0.0 if fresh else side[0]
-                for k in range(two):
-                    x = jnp.concatenate([lhs[0, k, i:i + CH, :], jnp.ones((16, lhs.shape[3]), BF16)], 0)
-                    v = rounded(k, x)
-                    z = z + v[:CH]
-                    e = e + v[CH:CH + 8]
-                side[0] = e
-            else:
-                for k in range(two):
-                    z = z + rounded(k, lhs[0, k, i:i + CH, :])
-            out[0, i:i + CH, :] = z
-            if not token_rows:
-                e = 0.0 if fresh else side[0, i:i + CH, :]
-                for k in range(two):
-                    v = lane_fold(lhs[0, k, i:i + CH, :].astype(F32))
-                    e = e + jnp.sum(v, axis=1, keepdims=True).astype(BF16).astype(F32)
-                side[0, i:i + CH, :] = jnp.broadcast_to(e, (CH, LANES))
-
-    @pl.when(m == 0)
-    def _():
-        go(True)
-
-    @pl.when(m > 0)
-    def _():
-        go(False)
-
-
-def weight_grad(lhs, rhs, token_rows, name):
-    c, n, rows, tok = lhs.shape
-    cols = rhs.shape[2]
-    two = 2
-    side = (8, cols) if token_rows else (rows, LANES)
+    )(dyt, *weights, *stash)
+
+
+PAIR = 2
+
+
+def grads_kernel(n, *refs):
+    ins, refs = refs[:8], refs[8:]
+    outs, bias_outs, refs = refs[:4], refs[4:7], refs[7:]
+    accs, biases, (buf, in_sems, out_sems) = refs[:4], refs[4:7], refs[7:]
+    steps = n // PAIR
+    tok = buf.shape[3]
+
+    def fetches(c, k, j):
+        slot = lax.rem(j, 2)
+        rows, cols = ins[2 * k].shape[2], ins[2 * k + 1].shape[2]
+        at = pl.ds(j * PAIR, PAIR)
+        return (pltpu.make_async_copy(ins[2 * k].at[c, at], buf.at[slot, :, pl.ds(0, rows), :], in_sems.at[slot, 0]),
+                pltpu.make_async_copy(ins[2 * k + 1].at[c, at], buf.at[slot, :, pl.ds(rows, cols), :], in_sems.at[slot, 1]))
+
+    def begin(c, k, j):
+        for cp in fetches(c, k, j):
+            cp.start()
+
+    def results(c, k):
+        cps = [pltpu.make_async_copy(accs[k], outs[k].at[c], out_sems.at[k])]
+        if k < 3:
+            cps.append(pltpu.make_async_copy(biases[k], bias_outs[k].at[c], out_sems.at[4 + k]))
+        return cps
+
+    begin(jnp.int32(0), 0, jnp.int32(0))
+
+    def stage(c, carry):
+        for k in range(4):
+            rows, cols = ins[2 * k].shape[2], ins[2 * k + 1].shape[2]
+
+            def step(j, carry, k=k, rows=rows, cols=cols):
+                @pl.when(j + 1 < steps)
+                def _():
+                    begin(c, k, j + 1)
+
+                @pl.when(j + 1 == steps)
+                def _():
+                    if k < 3:
+                        begin(c, k + 1, jnp.int32(0))
+                    else:
+                        @pl.when(c == 0)
+                        def _():
+                            begin(jnp.int32(1), 0, jnp.int32(0))
+
+                @pl.when(jnp.logical_and(j == 0, c == 1))
+                def _():
+                    for cp in results(jnp.int32(0), k):
+                        cp.wait()
+
+                for cp in fetches(c, k, j):
+                    cp.wait()
+                slot = lax.rem(j, 2)
+                later = j > 0
+                for i in range(0, rows, CH):
+                    z = jnp.where(later, accs[k][i:i + CH, :], 0.0)
+                    if i == 0 and k < 3:
+                        e = jnp.where(later, biases[k][...], 0.0)
+                    for q in range(PAIR):
+                        x = buf[slot, q, i:i + CH, :]
+                        if i == 0 and k < 3:
+                            x = jnp.concatenate([x, jnp.ones((16, tok), BF16)], 0)
+                        v = dot(x, buf[slot, q, rows:rows + cols, :], 1, 1).astype(BF16).astype(F32)
+                        z = z + v[:CH]
+                        if i == 0 and k < 3:
+                            e = e + v[CH:CH + 8]
+                    accs[k][i:i + CH, :] = z
+                    if i == 0 and k < 3:
+                        biases[k][...] = e
+                return carry
+
+            lax.fori_loop(0, steps, step, 0)
+            for cp in results(c, k):
+                cp.start()
+        return carry
+
+    lax.fori_loop(0, 2, stage, 0)
+    for k in range(4):
+        for cp in results(jnp.int32(1), k):
+            cp.wait()
+
+
+def run_grads(pairs):
+    n, tok = pairs[0][0].shape[1], pairs[0][0].shape[3]
+    sizes = [(a.shape[2], b.shape[2]) for a, b in pairs]
+    st = jax.ShapeDtypeStruct
+    vm = pltpu.VMEM
+    most = max(a + b for a, b in sizes)
     return pl.pallas_call(
-        functools.partial(weight_kernel, token_rows), grid=(c, n // two),
-        out_shape=[jax.ShapeDtypeStruct((c, rows, cols), F32), jax.ShapeDtypeStruct((c,) + side, F32)],
-        in_specs=[pl.BlockSpec((1, two, rows, tok), lambda i, j: (i, j, 0, 0)),
-                  pl.BlockSpec((1, two, cols, tok), lambda i, j: (i, j, 0, 0))],
-        out_specs=[pl.BlockSpec((1, rows, cols), lambda i, j: (i, 0, 0)),
-                   pl.BlockSpec((1,) + side, lambda i, j: (i, 0, 0))],
-        name=name,
-        compiler_params=pltpu.CompilerParams(vmem_limit_bytes=VMEM_LIMIT, dimension_semantics=('arbitrary', 'arbitrary')),
-    )(lhs, rhs)
+        functools.partial(grads_kernel, n),
+        out_shape=[st((2,) + v, F32) for v in sizes] + [st((2, 8, v[1]), F32) for v in sizes[:3]],
+        in_specs=[HBM] * 8, out_specs=[HBM] * 7,
+        scratch_shapes=[vm(v, F32) for v in sizes] + [vm((8, v[1]), F32) for v in sizes[:3]] + [
+            vm((2, PAIR, most, tok), BF16), pltpu.SemaphoreType.DMA((2, 2)), pltpu.SemaphoreType.DMA((7,))],
+        name='weight_grads', compiler_params=pltpu.CompilerParams(vmem_limit_bytes=VMEM_LIMIT),
+    )(*[v for p in pairs for v in p])
 
 
 def solution(mesh):
@@ -541,26 +617,21 @@
         heads = w_qkv.shape[5]
         tok = batch * seq
 
-        def column(v):
-            return jnp.broadcast_to(v[..., None], v.shape + (LANES,))
-
-        weights = (
-            w_qkv.reshape(2, d, 3 * d).transpose(0, 2, 1), w_attn.reshape(2, d, d), w_fc[0, :, 0], w_proj[0, :, 0],
-            column(b_qkv.reshape(2, 3 * d)), column(b_fc.reshape(2, -1)), column(vec_d[0, :, 0]))
+        cols = jnp.concatenate([vec_d[0, :, 0], b_qkv.reshape(2, 3, d), b_fc.reshape(2, -1, d)], axis=1)
+        cols = jnp.pad(cols.transpose(0, 2, 1), ((0, 0), (0, 0), (0, LANES - cols.shape[1])))
+        weights = (w_qkv.reshape(2, d, 3 * d).transpose(0, 2, 1), w_attn.reshape(2, d, d), w_fc[0, :, 0], w_proj[0, :, 0],
+                   cols)
         xt = x.reshape(tok, d).T
         dyt = dy.reshape(tok, d).T
         yt, hs, ts, rs, ps, gs, ss, as_, os_, bs, us = run_forward(mesh, heads, seq, xt, weights)
         dxt, dys, dgs, drs, dts, sums = run_backward(mesh, heads, seq, dyt, weights, (hs, ts, rs, ps, gs, ss))
-        gq, gbq = weight_grad(dts, as_, False, 'grad_qkv')
-        go, gbo = weight_grad(os_, drs, True, 'grad_attn')
-        g1, gb1 = weight_grad(bs, dgs, True, 'grad_fc')
-        g2, gb2 = weight_grad(us, dys, True, 'grad_proj')
-        s = sums[:, :, :4].transpose(0, 2, 1)
+        g1, g2, go, gq, gb1, gb2, gbo = run_grads(((bs, dgs), (us, dys), (os_, drs), (dts, as_)))
+        s = sums[:, :, :7].transpose(0, 2, 1)
         gv = jnp.stack([s[:, 0], s[:, 1], gbo[:, 0], s[:, 2], s[:, 3], gb2[:, 0]], axis=1)
         back = lambda v: v.T.reshape(x.shape)
         return (back(yt), back(dxt),
                 gq.transpose(0, 2, 1).reshape(w_qkv.shape), go.reshape(w_attn.shape), g1.reshape(w_fc.shape),
-                g2.reshape(w_proj.shape), gbq[:, :, 0].reshape(b_qkv.shape), gb1[:, 0].reshape(b_fc.shape),
+                g2.reshape(w_proj.shape), s[:, 4:7].reshape(b_qkv.shape), gb1[:, 0].reshape(b_fc.shape),
                 gv.reshape(vec_d.shape))
 
     return jax.shard_map(per_device, mesh=mesh, in_specs=(data_spec, data_spec) + (weight_spec,) * 7,

time: 955 us -> 869 us (0.910)
  Pallas kernels: 917 us -> 834 us
    pallas_call x1, Pallas kernels: 406 us -> 347 us  [run_forward(): pl.pallas_call(functools.partial(forward_kernel, n, heads, seq), out_shap...]
    pallas_call x4 -> x1, Pallas kernels: 160 us -> 147 us  [run_grads(): pl.pallas_call(functools.partial(grads_kernel, n), out_shape=[st((2,) + v...]
    pallas_call x1, Pallas kernels: 352 us -> 340 us  [run_backward(): pl.pallas_call(functools.partial(backward_kernel, n, heads, seq), out_sha...]
where the time goes in v2:
time: 869 us; the launch traced here: 856 us
  Pallas kernels  834 us (96%)
  local copies, waits for them, and re-layouts  20 us (2%)
    pallas_call x1, Pallas kernels, run_forward(): pl.pallas_call(functools.partial(forward_kernel, n, heads, seq), out_shap...  347 us
    pallas_call x1, Pallas kernels, run_backward(): pl.pallas_call(functools.partial(backward_kernel, n, heads, seq), out_sha...  340 us
    pallas_call x1, Pallas kernels, run_grads(): pl.pallas_call(functools.partial(grads_kernel, n), out_shape=[st((2,) + v...  147 us

profile of v2, /device:TPU:127, one launch (start us, length us, event | category | flops | bytes accessed | tf_op | source)
XLA Modules:
  0.0 855.6 jit_solution(2902907692626692713)
XLA Ops:
  0.6 0.7 reshape.64
  1.4 0.3 copy.67
  1.7 1.1 copy.66
  2.7 1.0 copy.65
  3.7 0.4 maximum_bitcast_fusion
  4.1 0.8 pad.4.cols
  4.9 2.3 copy.81
  7.2 2.3 copy.83
  9.5 346.8 %forward_walk.1 = (bf16[768,512]{1,0:T(8,128)(2,1)}, bf16[2,8,768,512]{3,2,1,0:T(8,128)(2,1)}, bf16[2,8,2304,512]{3,2,1,0:T(8,128)(2,1)}, bf16[2,8,768,512]{3,2,...) custom-call(bf16[768,512]{1,0:T(8,128)(2,1)} %bitcast.50, ...), custom_call_target="tpu_custom_call" | custom-call | tf_op jit(solution)/shard_map/forward_walk/pallas_call | solution.py:482
  356.2 2.3 copy.82
  358.5 340.0 %backward_walk.1 = (bf16[768,512]{1,0:T(8,128)(2,1)}, bf16[2,8,768,512]{3,2,1,0:T(8,128)(2,1)}, bf16[2,8,3072,512]{3,2,1,0:T(8,128)(2,1)}, bf16[2,8,768,512]{3,2...) custom-call(bf16[768,512]{1,0:T(8,128)(2,1)} %bitcast.51, bf16[2,2304,768]{2,1,0:T(8,128)(2,1)} %bitcast.46, ...), custom_call_target="tpu_custom_call" | custom-call | tf_op jit(solution)/shard_map/backward_walk/pallas_call | solution.py:504
  698.6 147.3 %weight_grads.1 = (f32[2,768,3072]{2,1,0:T(8,128)}, f32[2,3072,768]{2,1,0:T(8,128)}, f32[2,768,768]{2,1,0:T(8,128)}, f32[2,2304,768]{2,1,0:T(8,128)}, f32[2,8,30...) custom-call(bf16[2,8,768,512]{3,2,1,0:T(8,128)(2,1)} %get-tuple-element.41.refs_0_, ...), custom_call_target="tpu_custom_call" | custom-call | tf_op jit(solution)/shard_map/weight_grads/pallas_call | solution.py:601
  845.9 2.3 copy.84
  848.2 0.8 slice.29
  849.0 0.8 slice.31
  849.8 1.5 slice_bitcast_fusion.1
  851.3 1.2 slice_bitcast_fusion
  852.5 0.3 slice.32
  852.8 0.9 copy.79
  853.7 0.3 fusion
  854.0 0.3 copy.69
  854.2 0.3 copy.71
  854.5 0.7 copy.80
  (3 shorter events, 0.0 us)

commit v3 on v2

v3 whole, which is shorter than its diff:
```python
import functools

import jax
import jax.numpy as jnp
from jax import lax
from jax.experimental import pallas as pl
from jax.experimental.pallas import tpu as pltpu
from jax.sharding import PartitionSpec as P

EPS = 1e-5
F32 = jnp.float32
BF16 = jnp.bfloat16
LANES = 128
ROWS = 32
CH = 256
WIDE = 512
SKEW = 8
K0 = 0.7978845608028654
K1 = K0 * 0.044715
VMEM_LIMIT = 67043328
HBM = pl.BlockSpec(memory_space=pl.ANY)


def dot(lhs, rhs, lc=1, rc=0):
    return lax.dot_general(lhs, rhs, (((lc,), (rc,)), ((), ())), preferred_element_type=F32)


def rows_sum(v):
    r, t = v.shape
    return jnp.sum(v.reshape(r // 8, 8, t), axis=0)


def rounded(v):
    return v.astype(BF16).astype(F32)


def lane_fold(v):
    return functools.reduce(jnp.add, [v[:, k:k + LANES] for k in range(0, v.shape[1], LANES)])


def block_diag(a, b):
    z = jnp.zeros_like(a)
    return jnp.concatenate([jnp.concatenate([a, z], 1), jnp.concatenate([z, b], 1)], 0)


def f_norm(src, gain, shift, dst, stats, lo, hi):
    d = src.shape[1]
    at = lax.broadcasted_iota(jnp.int32, (ROWS, LANES), 1)
    for i in range(lo, hi, ROWS):
        x = src[i:i + ROWS, :].astype(F32)
        mean = jnp.sum(x, axis=1, keepdims=True) * (1.0 / d)
        x = x - mean
        rstd = lax.rsqrt(jnp.sum(x * x, axis=1, keepdims=True) * (1.0 / d) + EPS)
        dst[i:i + ROWS, :] = (x * rstd * gain + shift).astype(BF16)
        stats[i:i + ROWS, :] = jnp.where(at == 0, mean, rstd)


def b_norm(dn, src, gain, skip, dst, stats, lo, hi):
    d = src.shape[1]
    pg = pb = pr = jnp.zeros((8, d), F32)
    for i in range(lo, hi, ROWS):
        mean, rstd = stats[i:i + ROWS, 0:1], stats[i:i + ROWS, 1:2]
        c = (src[i:i + ROWS, :].astype(F32) - mean) * rstd
        v = dn(i, i + ROWS)
        pg += rows_sum(v * c)
        pb += rows_sum(v)
        g = v * gain
        m1 = jnp.sum(g, axis=1, keepdims=True) * (1.0 / d)
        m2 = jnp.sum(g * c, axis=1, keepdims=True) * (1.0 / d)
        z = ((g - m1 - c * m2) * rstd + skip[i:i + ROWS, :].astype(F32)).astype(BF16)
        dst[i:i + ROWS, :] = z
        pr += rows_sum(z.astype(F32))
    return pg, pb, pr


def skewed(jobs, first, second):
    pending = []

    def one(job):
        if job is not None:
            pending.append((job, first(*job)))
        if job is None or len(pending) > SKEW:
            j, v = pending.pop(0)
            second(*j, v)

    return [functools.partial(one, job) for job in jobs + [None] * min(SKEW, len(jobs))]


def f_heads(t, o, p, heads, seq, seqs, after):
    d = o.shape[0]
    head = d // heads
    two = 2 * head
    pairs = heads // 2
    c = (head ** -0.5) * 1.4426950408889634

    def score(b, j):
        r0, lanes = two * j, slice(b * seq, (b + 1) * seq)
        q = t[r0:r0 + two, lanes]
        return dot(t[d + r0:d + r0 + two, lanes], block_diag(q[:head], q[head:]), 0, 0)

    def mix(b, j, s):
        r0, lanes = two * j, slice(b * seq, (b + 1) * seq)
        key = lax.broadcasted_iota(jnp.int32, (seq, 2 * seq), 0)
        qry = lax.rem(lax.broadcasted_iota(jnp.int32, (seq, 2 * seq), 1), seq)
        s = jnp.where(key <= qry, s, -1e30)
        m = jnp.max(s, axis=0, keepdims=True)
        e = jnp.exp2((s - m) * c)
        e = e * (1.0 / jnp.sum(e, axis=0, keepdims=True))
        p[b * seq:(b + 1) * seq, 2 * seq * j:2 * seq * (j + 1)] = e
        x = dot(t[2 * d + r0:2 * d + r0 + two, lanes], e.astype(BF16))
        o[r0:r0 + head, lanes] = x[:head, :seq].astype(BF16)
        o[r0 + head:r0 + two, lanes] = x[head:, seq:].astype(BF16)
        if j == pairs - 1:
            after(b)

    return skewed([(b, j) for b in seqs for j in range(pairs)], score, mix)


def b_heads(t, do, p, heads, seq, seqs, after):
    d = do.shape[0]
    head = d // heads
    two = 2 * head
    pairs = heads // 2
    scale = head ** -0.5

    def first(b, j):
        r0, lanes = two * j, slice(b * seq, (b + 1) * seq)
        z = do[r0:r0 + two, lanes]
        return dot(t[2 * d + r0:2 * d + r0 + two, lanes], block_diag(z[:head], z[head:]), 0, 0)

    def diag(r0, lanes, x, k):
        t[r0:r0 + head, lanes] = (x[:head, :seq] * k).astype(BF16)
        t[r0 + head:r0 + two, lanes] = (x[head:, seq:] * k).astype(BF16)

    def second(b, j, dp):
        r0, lanes = two * j, slice(b * seq, (b + 1) * seq)
        e = p[b * seq:(b + 1) * seq, 2 * seq * j:2 * seq * (j + 1)]
        w = e * dp
        ds = (w - e * jnp.sum(w, axis=0, keepdims=True)).astype(BF16)
        eb = e.astype(BF16)
        q, k = t[r0:r0 + two, lanes], t[d + r0:d + r0 + two, lanes]
        tall = jnp.concatenate([ds[:, :seq], ds[:, seq:]], 0)
        dq, dk = dot(k, ds), dot(q, tall, 1, 1)
        tall = jnp.concatenate([eb[:, :seq], eb[:, seq:]], 0)
        dv = dot(do[r0:r0 + two, lanes], tall, 1, 1)
        diag(r0, lanes, dq, scale)
        diag(d + r0, lanes, dk, scale)
        diag(2 * d + r0, lanes, dv, 1.0)
        if j == pairs - 1:
            after(b)

    return skewed([(b, j) for b in seqs for j in range(pairs)], first, second)


def gelu_and_slope(x):
    x2 = x * x
    hp = 0.5 * jnp.tanh(x * (x2 * K1 + K0)) + 0.5
    u = x * hp
    return u, hp + (u - u * hp) * (x2 * (6.0 * K1) + 2.0 * K0)


def woven(*lists):
    total = max(len(v) for v in lists)
    done = [0] * len(lists)
    for k in range(total):
        for i, v in enumerate(lists):
            while done[i] * total < (k + 1) * len(v) and done[i] < len(v):
                v[done[i]]()
                done[i] += 1


class Group:
    def __init__(self, n):
        self.n, self.half, self.last = n, n // 2, n - 1
        self.me = lax.axis_index('pp')
        self.side = self.me // self.half
        self.depth = self.me + self.side * (self.last - 2 * self.me)
        self.inner = self.me + 1 - 2 * self.side
        self.outer = self.me - 1 + 2 * self.side
        self.lead = self.half + 1 - self.depth - self.depth // 2

    def place(self, i):
        far = lax.rem(i - self.half + self.half // 2, self.half) + self.half
        return jnp.where(i < self.half, i, far)

    def step(self, s):
        q = s - self.lead
        pair = q // 2
        even = (q - 2 * pair) == 0
        rest = self.n - self.lead
        head = s < self.lead
        alt = q < 2 * rest
        second = jnp.logical_and(jnp.logical_not(head), jnp.logical_or(jnp.logical_not(alt), even))
        m = jnp.where(head, s, jnp.where(alt, jnp.where(even, pair, self.lead + pair), q - rest))
        return second.astype(jnp.int32), m


def run_phase(g, c_first, src, final, slots, out, load_sems, recv_sems, send_sems, final_sem, feed_sems, weights, unit,
              begin=None):
    n, half = g.n, g.half
    inside = g.depth == half - 1
    outside = g.depth == 0

    def copies_of(c):
        return [pltpu.make_async_copy(h.at[c], v.at[c], load_sems.at[c, i]) for i, (h, v) in enumerate(weights)]

    for c in (c_first, 1 - c_first):
        for w in copies_of(c):
            w.start()
    barrier = pltpu.get_barrier_semaphore()
    for i in range(n):
        pl.semaphore_signal(barrier, inc=1, device_id={'pp': jnp.int32(i)})
    pl.semaphore_wait(barrier, n)
    if begin is not None:
        begin()

    def remote(a, b, send, recv, dev):
        return pltpu.make_async_remote_copy(src_ref=a, dst_ref=b, send_sem=send, recv_sem=recv, device_id={'pp': dev})

    for k, head in ((0, 0), (1, g.last)):
        spot = g.place(g.me + k * (g.last - 2 * g.me))

        @pl.when(g.me == head)
        def _():
            pltpu.make_async_copy(src, slots.at[0, spot], recv_sems.at[0, spot]).start()

        @pl.when(g.me != head)
        def _():
            remote(src, slots.at[0, spot], feed_sems.at[k], recv_sems.at[0, spot], jnp.int32(head)).start()

    def sent(s):
        sec, m = g.step(s)
        kept = jnp.logical_or(jnp.logical_and(sec == 0, inside),
                              jnp.logical_and(jnp.logical_and(sec == 1, outside), m >= half))
        return jnp.logical_not(kept)

    def settle(s):
        @pl.when(sent(s))
        def _():
            par = lax.rem(s, 2)
            remote(out.at[par], slots.at[0, 0], send_sems.at[par], recv_sems.at[0, 0], g.me).wait_send()

    def body(s, carry):
        sec, m = g.step(s)
        c = jnp.where(sec == 1, 1 - c_first, c_first)
        par = lax.rem(s, 2)

        @pl.when(jnp.logical_or(s == 0, s == g.lead))
        def _():
            for w in copies_of(c):
                w.wait()

        @pl.when(s >= 2)
        def _():
            settle(s - 2)

        @pl.when(jnp.logical_not(jnp.logical_and(sec == 1, inside)))
        def _():
            remote(out.at[par], slots.at[sec, m], send_sems.at[par], recv_sems.at[sec, m], g.me).wait_recv()

        unit(s, c, m, slots.at[sec, m], out.at[par])

        @pl.when(jnp.logical_and(sec == 0, inside))
        def _():
            slots[1, m] = out[par]

        @pl.when(jnp.logical_and(sec == 0, jnp.logical_not(inside)))
        def _():
            remote(out.at[par], slots.at[0, m], send_sems.at[par], recv_sems.at[0, m], g.inner).start()

        @pl.when(jnp.logical_and(sec == 1, jnp.logical_not(outside)))
        def _():
            remote(out.at[par], slots.at[1, m], send_sems.at[par], recv_sems.at[1, m], g.outer).start()

        owner = m + g.side * (g.last - 2 * m)
        done = jnp.logical_and(jnp.logical_and(sec == 1, outside), m < half)

        @pl.when(jnp.logical_and(done, owner == g.me))
        def _():
            pltpu.make_async_copy(out.at[par], final, send_sems.at[par]).start()

        @pl.when(jnp.logical_and(done, owner != g.me))
        def _():
            remote(out.at[par], final, send_sems.at[par], final_sem.at[0], owner).start()

        return carry

    lax.fori_loop(0, 2 * n, body, 0)
    settle(2 * n - 2)
    settle(2 * n - 1)
    for k, head in ((0, 0), (1, g.last)):
        @pl.when(g.me != head)
        def _():
            remote(src, slots.at[0, 0], feed_sems.at[k], recv_sems.at[0, 0], jnp.int32(head)).wait_send()

    @pl.when(jnp.logical_not(outside))
    def _():
        remote(out.at[0], final, send_sems.at[0], final_sem.at[0], g.me).wait_recv()


def forward_kernel(n, heads, seq, src, wq, wo, w1, w2, cols, rows, b1,
                   final, hs, ts, rs, ps, gs, ss, as_, os_, bs, us,
                   vwq, vwo, vw1, vw2, vcols, vrows, vb1, slots, out, a, bb, t, o, r, u, p, gp, ya, stats,
                   load_sems, recv_sems, send_sems, final_sem, feed_sems, sems):
    g = Group(n)
    tok, d = a.shape
    f = u.shape[1]
    half = tok // 2

    def unit(s, c, m, x, y):
        def copy(i, v, dst, at=None):
            hbm = dst.at[c, m]
            if at is not None:
                v, hbm = v.at[at], hbm.at[at]
            return pltpu.make_async_copy(v, hbm, sems.at[i])

        def vec(k):
            return vrows[c, k:k + 1, :]

        def norm1(q):
            f_norm(x, vec(0), vec(1), a, stats.at[0], q * half, (q + 1) * half)
            copy(1, a, as_, (pl.ds(q * half, half),)).start()

        def project(q, i):
            z = dot(vwq[c, i:i + CH, :], a[q * half:(q + 1) * half, :], 1, 1)
            z = z + vcols[c, i % d:i % d + CH, i // d:i // d + 1].astype(F32)
            t[i:i + CH, q * half:(q + 1) * half] = z.astype(BF16)

        def attend(q):
            seqs = range(q * half // seq, (q + 1) * half // seq)
            return f_heads(t, o, p, heads, seq, seqs, lambda b: copy(4, p, ps, (pl.ds(b * seq, seq),)).start())

        def merge(q):
            for i in range(q * half, (q + 1) * half, LANES):
                z = dot(o[:, i:i + LANES], vwo[c], 0, 0) + vec(2) + x[i:i + LANES, :].astype(F32)
                z = z.astype(BF16)
                r[i:i + LANES, :] = z
                ya[i:i + LANES, :] = z.astype(F32) + vec(5)

        def norm2(q):
            f_norm(r, vec(3), vec(4), bb, stats.at[1], q * half, (q + 1) * half)
            copy(5, r, rs, (pl.ds(q * half, half),)).start()
            copy(6, bb, bs, (pl.ds(q * half, half),)).start()

        def up(q, j):
            rs_, cs = slice(q * half, (q + 1) * half), slice(j, j + WIDE)
            h = dot(bb[rs_, :], vw1[c, :, cs]) + vb1[c, 0:1, cs]
            uu, slope = gelu_and_slope(h)
            u[rs_, cs] = uu.astype(BF16)
            gp[rs_, cs] = slope
            at = (pl.ds(q * half, half), pl.ds(j, WIDE))
            copy(8, u, us, at).start()
            copy(9, gp, gs, at).start()

        def down(q, j):
            rs_ = slice(q * half, (q + 1) * half)
            ks = slice(j, j + 2 * WIDE)

            def add(rs_, cs):
                z = ya[rs_, cs] + dot(u[rs_, ks], vw2[c, ks, cs])
                if j + 2 * WIDE < f:
                    ya[rs_, cs] = z
                else:
                    y[rs_, cs] = z.astype(BF16)

            add(rs_, slice(0, WIDE))
            add(slice(q * half, q * half + LANES), slice(WIDE, d))
            add(slice(q * half + LANES, (q + 1) * half), slice(WIDE, d))

        def each(fn, q, hi, step):
            return [functools.partial(fn, q, i) for i in range(0, hi, step)]

        copy(0, x, hs).start()
        norm1(0)
        first = each(project, 0, 3 * d, CH)
        woven(first[:2])
        norm1(1)
        woven(first[2:])
        woven(attend(0), each(project, 1, 3 * d, CH))
        copy(2, t, ts).start()
        merge(0)
        late = attend(1)
        woven(late[:4], [functools.partial(norm2, 0)])
        woven(late[4:], each(up, 0, f, WIDE))
        copy(3, o, os_).start()
        merge(1)
        ups, downs = each(up, 1, f, WIDE), each(down, 0, f, 2 * WIDE)
        woven([downs[0]], [functools.partial(norm2, 1)])
        woven(ups, downs[1:])
        woven(each(down, 1, f, 2 * WIDE))
        copy(7, stats, ss).start()
        for i, v, dst in ((0, x, hs), (1, a, as_), (2, t, ts), (3, o, os_), (4, p, ps), (5, r, rs), (6, bb, bs),
                          (7, stats, ss), (8, u, us), (9, gp, gs)):
            copy(i, v, dst).wait()

    weights = [(wq, vwq), (wo, vwo), (w1, vw1), (w2, vw2), (cols, vcols), (rows, vrows), (b1, vb1)]
    run_phase(g, g.side, src, final, slots, out, load_sems, recv_sems, send_sems, final_sem, feed_sems, weights, unit)


def backward_kernel(n, heads, seq, src, wq, wo, w1, w2, rows, hs, ts, rs, ps, gs, ss,
                    final, dys, dgs, drs, dts, sum_rows, sum_b1, sum_bq,
                    vwq, vwo, vw1, vw2, vrows, slots, out, h, t, r, dg, dr, do, pg, stats, acc_rows, acc_b1, acc_bq, part,
                    load_sems, recv_sems, send_sems, final_sem, feed_sems, in_sems, sems):
    g = Group(n)
    tok, d = h.shape
    f = dg.shape[1]
    half = tok // 2
    pcol = ps.shape[3]
    c_first = 1 - g.side

    def fetch(i, s, at=None):
        sec, m = g.step(s)
        c = jnp.where(sec == 1, 1 - c_first, c_first)
        hbm, v = ((gs, pg), (ps, pg.at[:, pl.ds(0, pcol)]), (ts, t), (rs, r), (hs, h), (ss, stats))[i]
        hbm = hbm.at[c, m]
        if at is not None:
            hbm, v = hbm.at[at], v.at[at]
        return pltpu.make_async_copy(hbm, v, in_sems.at[i])

    def ahead(i, s, at=None):
        @pl.when(s + 1 < 2 * n)
        def _():
            fetch(i, s + 1, at).start()

    for i in (0, 2, 3, 4, 5):
        fetch(i, 0).start()
    for v in (acc_rows, acc_b1, acc_bq):
        v[...] = jnp.zeros_like(v)

    def unit(s, c, m, dy, y):
        def copy(i, v, dst):
            return pltpu.make_async_copy(v, dst.at[c, m], sems.at[i])

        def vec(k):
            return vrows[c, k:k + 1, :]

        def down(j):
            cs = slice(j, j + WIDE)
            w = rounded(dot(dy[...], vw2[c, cs, :], 1, 1)) * pg[:, cs]
            dg[:, cs] = w.astype(BF16)
            acc_b1[c, 0:1, cs] += rounded(jnp.sum(rows_sum(w), axis=0, keepdims=True))

        def up(i):
            y[:, i:i + CH] = dot(vw1[c, i:i + CH, :], dg[...], 1, 1).astype(BF16).T

        def tally(k, v):
            acc_rows[c, k:k + 1, :] += rounded(jnp.sum(v, axis=0, keepdims=True))

        def norm(q, src, k, skip, dst, st):
            sums = b_norm(lambda i, e: y[i:e, :].astype(F32), src, vec(k), skip, dst, st, q * half, (q + 1) * half)
            for i, v in enumerate(sums if k else sums[:2]):
                if q == 0:
                    part[i] = v
                else:
                    tally((k, k + 1, 2)[i], part[i] + v)

        def unmerge(q):
            qs = slice(q * half, (q + 1) * half)
            for i in range(0, d, CH):
                do[i:i + CH, qs] = dot(vwo[c, i:i + CH, :], dr[qs, :], 1, 1).astype(BF16)

        def attend(q):
            seqs = range(q * half // seq, (q + 1) * half // seq)
            return b_heads(t, do, pg, heads, seq, seqs, lambda b: ahead(0, s, (pl.ds(b * seq, seq), pl.ds(0, pcol))))

        def unproject(q, i):
            y[i:i + LANES, :] = dot(t[:, i:i + LANES], vwq[c], 0, 0).astype(BF16)

        def bias_q(i):
            at = lax.broadcasted_iota(jnp.int32, (ROWS, LANES), 1)
            e = 0.0
            for k in range(3):
                w = lane_fold(t[k * d + i:k * d + i + ROWS, :].astype(F32))
                e = jnp.where(at == k, rounded(jnp.sum(w, axis=1, keepdims=True)), e)
            acc_bq[c, i:i + ROWS, :] += e

        copy(0, dy, dys).start()
        fetch(0, s).wait()
        woven([functools.partial(down, j) for j in range(0, f, WIDE)])
        fetch(1, s).start()
        ahead(0, s, (slice(None), pl.ds(pcol, f - pcol)))
        copy(1, dg, dgs).start()
        tally(5, rows_sum(dy[...].astype(F32)))
        woven([functools.partial(up, i) for i in range(0, d, CH)])
        fetch(3, s).wait()
        fetch(5, s).wait()
        norm(0, r, 3, dy, dr, stats.at[1])
        unmerge(0)
        norm(1, r, 3, dy, dr, stats.at[1])
        ahead(3, s)
        copy(2, dr, drs).start()
        fetch(1, s).wait()
        fetch(2, s).wait()
        woven(attend(0), [functools.partial(unmerge, 1)])
        fetch(4, s).wait()
        woven(attend(1), [functools.partial(unproject, 0, i) for i in range(0, half, LANES)])
        copy(3, t, dts).start()
        norm(0, h, 0, dr, y, stats.at[0])
        woven([functools.partial(unproject, 1, i) for i in range(half, tok, LANES)])
        woven([functools.partial(bias_q, i) for i in range(0, d, ROWS)])
        norm(1, h, 0, dr, y, stats.at[0])
        ahead(4, s)
        ahead(5, s)
        for i, v, dst in ((0, dy, dys), (1, dg, dgs), (2, dr, drs), (3, t, dts)):
            copy(i, v, dst).wait()
        ahead(2, s)

    weights = [(wq, vwq), (wo, vwo), (w1, vw1), (w2, vw2), (rows, vrows)]
    run_phase(g, c_first, src, final, slots, out, load_sems, recv_sems, send_sems, final_sem, feed_sems, weights, unit)
    cps = [pltpu.make_async_copy(v, o, sems.at[i])
           for i, (v, o) in enumerate(((acc_rows, sum_rows), (acc_b1, sum_b1), (acc_bq, sum_bq)))]
    for cp in cps:
        cp.start()
    for cp in cps:
        cp.wait()


def walk(kernel, name, number, outs, scratch, args):
    return pl.pallas_call(
        kernel, out_shape=outs, in_specs=[HBM] * len(args), out_specs=[HBM] * len(outs), scratch_shapes=scratch, name=name,
        compiler_params=pltpu.CompilerParams(vmem_limit_bytes=VMEM_LIMIT, collective_id=number, has_side_effects=True),
    )(*args)


def semaphores(n, weights, local):
    dma = pltpu.SemaphoreType.DMA
    return [dma((2, weights)), dma((2, n)), dma((2,)), dma((1,)), dma((2,))] + [dma((k,)) for k in local]


def run_forward(n, heads, seq, x, weights):
    tok, d = x.shape
    f = weights[2].shape[2]
    pcol = heads * seq
    vm, st = pltpu.VMEM, jax.ShapeDtypeStruct
    shapes = (((tok, d), BF16), ((3 * d, tok), BF16), ((tok, d), BF16), ((tok, pcol), F32), ((tok, f), F32),
              ((2, tok, LANES), F32), ((tok, d), BF16), ((d, tok), BF16), ((tok, d), BF16), ((tok, f), BF16))
    outs = [st((tok, d), BF16)] + [st((2, n) + v, k) for v, k in shapes]
    scratch = [vm(w.shape, w.dtype) for w in weights] + [
        vm((2, n, tok, d), BF16), vm((2, tok, d), BF16), vm((tok, d), BF16), vm((tok, d), BF16), vm((3 * d, tok), BF16),
        vm((d, tok), BF16), vm((tok, d), BF16), vm((tok, f), BF16), vm((tok, pcol), F32), vm((tok, f), F32),
        vm((tok, d), F32), vm((2, tok, LANES), F32)] + semaphores(n, len(weights), (10,))
    return walk(functools.partial(forward_kernel, n, heads, seq), 'forward_walk', 0, outs, scratch, (x, *weights))


def run_backward(n, heads, seq, dy, weights, stash):
    tok, d = dy.shape
    f = weights[2].shape[2]
    vm, st = pltpu.VMEM, jax.ShapeDtypeStruct
    outs = [st((tok, d), BF16)] + [st((2, n) + v, BF16) for v in ((tok, d), (tok, f), (tok, d), (3 * d, tok))]
    sums = [((2, 8, d), F32), ((2, 8, f), F32), ((2, d, LANES), F32)]
    outs += [st(*v) for v in sums]
    scratch = [vm(w.shape, w.dtype) for w in weights] + [
        vm((2, n, tok, d), BF16), vm((2, tok, d), BF16), vm((tok, d), BF16), vm((3 * d, tok), BF16), vm((tok, d), BF16),
        vm((tok, f), BF16), vm((tok, d), BF16), vm((d, tok), BF16), vm((tok, f), F32), vm((2, tok, LANES), F32)] + [
        vm(*v) for v in sums] + [vm((3, 8, d), F32)] + semaphores(n, len(weights), (6, 4))
    return walk(functools.partial(backward_kernel, n, heads, seq), 'backward_walk', 1, outs, scratch, (dy, *weights, *stash))


PAIR = 2


def grads_kernel(n, sides, *refs):
    ins, outs, accs, (broad, narrow, tall, in_sems, out_sems) = refs[:8], refs[8:12], refs[12:16], refs[16:]
    steps = n // PAIR
    short = tall.at[:, :, pl.ds(0, ins[4].shape[2]), :]
    bufs = ((narrow, broad), (broad, narrow), (short, narrow), (tall, narrow))

    def fetches(c, k, j):
        slot = lax.rem(j, 2)
        at = pl.ds(j * PAIR, PAIR)
        return [pltpu.make_async_copy(ins[2 * k + i].at[c, at], bufs[k][i].at[slot], in_sems.at[slot, i]) for i in range(2)]

    def begin(c, k, j):
        for cp in fetches(c, k, j):
            cp.start()

    def result(c, k):
        return pltpu.make_async_copy(accs[k], outs[k].at[c], out_sems.at[k])

    begin(jnp.int32(0), 0, jnp.int32(0))

    def stage(c, carry):
        for k in range(4):
            def step(j, carry, k=k):
                @pl.when(j + 1 < steps)
                def _():
                    begin(c, k, j + 1)

                @pl.when(j + 1 == steps)
                def _():
                    if k < 3:
                        begin(c, k + 1, jnp.int32(0))
                    else:
                        @pl.when(c == 0)
                        def _():
                            begin(jnp.int32(1), 0, jnp.int32(0))

                @pl.when(jnp.logical_and(j == 0, c == 1))
                def _():
                    result(jnp.int32(0), k).wait()

                for cp in fetches(c, k, j):
                    cp.wait()
                slot = lax.rem(j, 2)
                later = j > 0
                lhs, rhs = bufs[k]
                for i in range(0, accs[k].shape[0], CH):
                    z = jnp.where(later, accs[k][i:i + CH, :], 0.0)
                    for q in range(PAIR):
                        x = lhs[slot, q, :, i:i + CH] if sides[k] == 0 else lhs[slot, q, i:i + CH, :]
                        z = z + rounded(dot(x, rhs[slot, q], sides[k], 0))
                    accs[k][i:i + CH, :] = z
                return carry

            lax.fori_loop(0, steps, step, 0)
            result(c, k).start()
        return carry

    lax.fori_loop(0, 2, stage, 0)
    for k in range(4):
        result(jnp.int32(1), k).wait()


def run_grads(pairs, sides):
    n = pairs[0][0].shape[1]
    st, vm = jax.ShapeDtypeStruct, pltpu.VMEM
    sizes = [(a.shape[3 - s], b.shape[3]) for (a, b), s in zip(pairs, sides)]
    bufs = [vm((2, PAIR) + v.shape[2:], BF16) for v in (pairs[0][1], pairs[0][0], pairs[3][0])]
    return pl.pallas_call(
        functools.partial(grads_kernel, n, sides), out_shape=[st((2,) + v, F32) for v in sizes],
        in_specs=[HBM] * 8, out_specs=[HBM] * 4,
        scratch_shapes=[vm(v, F32) for v in sizes] + bufs + [pltpu.SemaphoreType.DMA((2, 2)), pltpu.SemaphoreType.DMA((4,))],
        name='weight_grads', compiler_params=pltpu.CompilerParams(vmem_limit_bytes=VMEM_LIMIT),
    )(*[v for p in pairs for v in p])


def solution(mesh):
    data_spec = P(('dp', 'pp'))
    weight_spec = P('pp')

    def per_device(x, dy, w_qkv, w_attn, w_fc, w_proj, b_qkv, b_fc, vec_d):
        _, batch, seq, d = x.shape
        heads = w_qkv.shape[5]
        tok = batch * seq

        n = mesh.shape['pp']
        cols = jnp.pad(b_qkv.reshape(2, 3, d).transpose(0, 2, 1), ((0, 0), (0, 0), (0, LANES - 3)))
        rows = jnp.pad(vec_d[0, :, 0].astype(F32), ((0, 0), (0, 2), (0, 0)))
        b1 = jnp.pad(b_fc.reshape(2, 1, -1).astype(F32), ((0, 0), (0, 7), (0, 0)))
        ws = (w_qkv.reshape(2, d, 3 * d).transpose(0, 2, 1), w_attn.reshape(2, d, d), w_fc[0, :, 0], w_proj[0, :, 0])
        y, hs, ts, rs, ps, gs, ss, as_, os_, bs, us = run_forward(n, heads, seq, x.reshape(tok, d), (*ws, cols, rows, b1))
        dx, dys, dgs, drs, dts, s_rows, s_b1, s_bq = run_backward(n, heads, seq, dy.reshape(tok, d), (*ws, rows),
                                                                  (hs, ts, rs, ps, gs, ss))
        g1, g2, go, gq = run_grads(((bs, dgs), (us, dys), (os_, drs), (dts, as_)), (0, 0, 1, 1))
        return (y.reshape(x.shape), dx.reshape(x.shape),
                gq.transpose(0, 2, 1).reshape(w_qkv.shape), go.reshape(w_attn.shape), g1.reshape(w_fc.shape),
                g2.reshape(w_proj.shape), s_bq[:, :, :3].transpose(0, 2, 1).reshape(b_qkv.shape),
                s_b1[:, 0].reshape(b_fc.shape), s_rows[:, :6].reshape(vec_d.shape))

    return jax.shard_map(per_device, mesh=mesh, in_specs=(data_spec, data_spec) + (weight_spec,) * 7,
                         out_specs=(data_spec, data_spec) + (data_spec,) * 7, check_vma=False)
```

time: 869 us -> 922 us (1.061)
  Pallas kernels: 834 us -> 894 us
    pallas_call x3, Pallas kernels: 834 us -> 894 us  [the longest x2 747 us: walk(): pl.pallas_call(kernel, out_shape=outs, in_specs=[HBM] * len(args), out_sp...]
where the time goes in v3:
time: 922 us; the launch traced here: 909 us
  Pallas kernels  894 us (97%)
  local copies, waits for them, and re-layouts  12.5 us (1%)
    pallas_call x2, Pallas kernels, walk(): pl.pallas_call(kernel, out_shape=outs, in_specs=[HBM] * len(args), out_sp...  747 us
    pallas_call x1, Pallas kernels, run_grads(): pl.pallas_call(functools.partial(grads_kernel, n, sides), out_shape=[st((...  147 us

profile of v3, /device:TPU:127, one launch (start us, length us, event | category | flops | bytes accessed | tf_op | source)
XLA Modules:
  0.0 908.7 jit_solution(1252394777285961022)
XLA Ops:
  0.6 0.7 copy.28
  1.4 0.7 copy.36
  2.1 0.6 pad_convert_fusion.1.rows
  2.7 0.7 pad_convert_fusion.b1
  3.4 1.0 copy.26
  4.5 0.8 pad.16.cols
  5.3 346.6 %forward_walk.1 = (bf16[512,768]{1,0:T(8,128)(2,1)}, bf16[2,8,512,768]{3,2,1,0:T(8,128)(2,1)}, bf16[2,8,2304,512]{3,2,1,0:T(8,128)(2,1)}, bf16[2,8,512,768]{3,2,...) custom-call(bf16[512,768]{1,0:T(8,128)(2,1)} %bitcast.51, ...), custom_call_target="tpu_custom_call" | custom-call | tf_op jit(solution)/shard_map/forward_walk/pallas_call | solution.py:519
  351.9 400.3 %backward_walk.1 = (bf16[512,768]{1,0:T(8,128)(2,1)}, bf16[2,8,512,768]{3,2,1,0:T(8,128)(2,1)}, bf16[2,8,512,3072]{3,2,1,0:T(8,128)(2,1)}, bf16[2,8,512,768]{3,2...) custom-call(bf16[512,768]{1,0:T(8,128)(2,1)} %bitcast.52, ...), custom_call_target="tpu_custom_call" | custom-call | tf_op jit(solution)/shard_map/backward_walk/pallas_call | solution.py:519
  752.2 146.9 %weight_grads.1 = (f32[2,768,3072]{2,1,0:T(8,128)}, f32[2,3072,768]{2,1,0:T(8,128)}, f32[2,768,768]{2,1,0:T(8,128)}, f32[2,2304,768]{2,1,0:T(8,128)}) custom-call(bf16[2,8,512,768]{3,2,1,0:T(8,128)(2,1)} %get-tuple-element.40.refs_0_, bf16[2,8,512,3072]{3,2,1,0:T(8,128)(2,1)} %get-tuple-element.41.refs_1_, ...), custom_call_target="tpu_custom_call" | custom-call | tf_op jit(solution)/shard_map/weight_grads/pallas_call | solution.py:629
  899.1 1.5 slice_bitcast_fusion.1
  900.6 2.1 copy.33
  902.7 0.8 slice_bitcast_fusion
  903.5 0.7 copy.34
  904.2 2.1 copy.39
  906.2 2.1 copy.40
